TPU v7x, 256 devices: a whole 4x4x8 slice. The times are simulated.
256 devices in a mesh: row: 4 (over y_lo, core), phi: 64 (over x, y_hi, z).
Axes of the slice: x: 4, y: 4 (y_hi: 2, y_lo: 2; y = y_hi * 2 + y_lo), z: 8, core: 2. Of those that a mesh axis runs over, the one named last changes fastest.
Arguments:
- hydro_vars: float32 [5, 128, 1024, 256], P(None, 'row', 'phi'), may hold values from -6 to 6
- face_b: float32 [3, 128, 1024, 256], P(None, 'row', 'phi'), may hold values from -6 to 6
- widths: int32 [16], replicated, may hold values from 2 to 1024, as said below
- diffusion: float32 [5, 256], replicated, may hold values from 0.01 to 0.06
Outputs:
- conserved: float32 [8, 128, 1024, 256], P(None, 'row', 'phi')
- faces_out: float32 [3, 128, 1024, 256], P(None, 'row', 'phi')
Inputs may be any that keep to these rules, and one draw needn't show every extreme that they name: `widths`: every width is a power of two that divides 1024; the two cycles next to the poles (entries 0 and 15) use 1024.
All inputs are finite; a program needn't handle non-finite values.
Results may differ from a plain program's by a relative error of at most 0.0001.
Values sent between devices are 32-bit elements; how exact they have to be, the bound alone decides.
A program may use at most 64 MiB of HBM per device.

v0:
```python
import jax
import jax.numpy as jnp
from jax import lax
from jax.sharding import PartitionSpec as P

CYCLES = 8


def extended(cells, sides, width, closed):
    for axis, dim in sides:
        count = lax.axis_size(axis)
        ends = count if closed else count - 1
        head = lax.slice_in_dim(cells, 0, width, axis=dim)
        tail = lax.slice_in_dim(cells, cells.shape[dim] - width, cells.shape[dim], axis=dim)
        cells = jnp.concatenate(
            [
                lax.ppermute(tail, axis, [(i, (i + 1) % count) for i in range(ends)]),
                cells,
                lax.ppermute(head, axis, [((i + 1) % count, i) for i in range(ends)]),
            ],
            axis=dim,
        )
    return cells


def passed_along(value, axis, steps):
    count = lax.axis_size(axis)
    initial, last = (max(0, -steps), min(count, count - steps))
    return lax.ppermute(value, axis, [(source, source + steps) for source in range(initial, last)])


def passed_along_2(block, axis, distance):
    devices = range(lax.axis_size(axis))
    route = [((i - distance) % len(devices), i) for i in devices]
    return lax.ppermute(block, axis, route)


def stencil(padded, axis, count):
    parts = [lax.slice_in_dim(padded, offset, offset + count, axis=axis) for offset in range(5)]
    return (16.0 * (parts[1] + parts[3]) - (parts[0] + parts[4]) - 30.0 * parts[2]) / 12.0


def block_means(cycles, axis, width, limit):
    cells = cycles.shape[axis]
    result = cycles
    for power in range(1, limit.bit_length()):
        size = 2**power
        shape = cycles.shape[:axis] + (cells // size, size) + cycles.shape[axis + 1 :]
        means = jnp.mean(cycles.reshape(shape), axis=axis + 1, keepdims=True)
        means = jnp.broadcast_to(means, shape).reshape(cycles.shape)
        result = jnp.where(width == size, means, result)
    return result


def body(hydro_vars, face_b, widths, diffusion):
    fields = jnp.concatenate([hydro_vars, face_b], 0)
    nfield, rows, cells, theta_cells = fields.shape
    cycle_count = 2 * CYCLES
    polar_cycles = jnp.concatenate([fields[..., :CYCLES], fields[..., theta_cells - CYCLES :]], 3)
    slab = polar_cycles.transpose(2, 0, 1, 3).reshape(cells, nfield * rows * cycle_count)
    whole = lax.all_to_all(slab, "phi", split_axis=1, concat_axis=0, tiled=True)
    columns = whole.shape[1]
    first = lax.axis_index("phi") * columns
    cycle_of = (first + jnp.arange(columns, dtype=jnp.int32)) % cycle_count
    match = cycle_of[:, None] == jnp.arange(cycle_count, dtype=jnp.int32)[None, :]
    column_width = jnp.sum(jnp.where(match, widths[None, :], 0), axis=1)
    means = block_means(whole, 0, column_width[None, :], whole.shape[0])
    back = lax.all_to_all(means, "phi", split_axis=0, concat_axis=1, tiled=True)
    averaged = back.reshape(cells, nfield, rows, cycle_count).transpose(1, 2, 0, 3)
    fields = jnp.concatenate(
        [
            averaged[..., :CYCLES],
            fields[..., CYCLES : theta_cells - CYCLES],
            averaged[..., CYCLES:],
        ],
        3,
    )
    hydro = fields[:5]
    radial_pad = extended(hydro, (("row", 1),), 2, False)
    azimuth_pad = extended(hydro, (("phi", 2),), 2, True)
    change_radial = stencil(radial_pad, 1, rows)
    change_azimuth = stencil(azimuth_pad, 2, cells)
    outer_layer = passed_along(fields[5, :1], "row", -1)
    radial_next = jnp.concatenate([fields[5, 1:], outer_layer], 0)
    after_layer = passed_along_2(fields[7, :, :1], "phi", -1)
    azimuth_next = jnp.concatenate([fields[7, :, 1:], after_layer], 1)
    theta_pad = jnp.pad(hydro, ((0, 0), (0, 0), (0, 0), (2, 2)))
    change = change_radial + change_azimuth + stencil(theta_pad, 3, theta_cells)
    smoothed = hydro + diffusion[:, None, None, :] * change
    polar_face = fields[6]
    polar_next = jnp.concatenate([polar_face[..., 1:], jnp.zeros_like(polar_face[..., :1])], 2)
    cell_field = 0.5 * jnp.stack(
        [fields[5] + radial_next, polar_face + polar_next, fields[7] + azimuth_next]
    )
    return (jnp.concatenate([smoothed, cell_field], 0), fields[5:])


def solution(mesh):
    in_specs = (P(None, "row", "phi", None), P(None, "row", "phi", None), P(), P())
    out_specs = (P(None, "row", "phi", None), P(None, "row", "phi", None))
    return jax.shard_map(body, mesh=mesh, in_specs=in_specs, out_specs=out_specs, check_vma=False)
```

profile of v0, /device:TPU:1, one launch (start us, length us, event | category | flops | bytes accessed | tf_op | source)
XLA Modules:
  0.0 108.5 jit_solution(15071981102177629928)
XLA Ops:
  0.6 2.1 %constant_dynamic-update-slice_fusion.1 = f32[8,32,16,256]{3,2,1,0:T(8,128)S(1)} fusion(f32[5,32,16,256]{3,2,1,0:T(8,128)} %param.4), kind=kLoop, calls=%fused_computation.76 | loop fusion | bytes 5242880
  2.7 0.1 copy-done.3
  2.8 0.1 constant_dynamic-update-slice_fusion
  2.9 0.0 copy-start.2
  3.0 0.7 fusion.32
  3.7 1.3 %copy-done.2 = f32[8,32,16,256]{3,2,1,0:T(8,128)} copy-done((f32[8,32,16,256]{3,2,1,0:T(8,128)}, f32[8,32,16,256]{3,2,1,0:T(8,128)S(1)}, u32[]{:S(2)}) %copy-start.2) | copy-done | bytes 4194328
  5.0 0.6 maximum_bitcast_fusion
  5.6 0.7 copy.37
  6.3 0.0 copy-start.5
  6.3 0.5 all_to_all.22
  6.8 0.3 copy.47
  7.1 1.0 reshape.250
  8.1 15.1 %all-to-all-start = ((f32[64,1,1024]{2,1,0:T(1,128)}), f32[64,1,1024]{2,1,0:T(1,128)S(1)}, u32[]{:S(2)}, u32[]{:S(2)}) async-start(f32[64,1,1024]{2,1,0:T(1,128)} %reshape.250), calls=%async_computation | async-start | bytes 524288 | tf_op jit(solution)/shard_map/all_to_all | solution.py:61
  23.2 0.1 select_reduce_fusion
  23.3 13.0 %all-to-all-done = f32[64,1,1024]{2,1,0:T(1,128)S(1)} async-done(((f32[64,1,1024]{2,1,0:T(1,128)}), f32[64,1,1024]{2,1,0:T(1,128)S(1)}, u32[]{:S(2)}, u32[]{:S(2)}) %all-to-all-start) | async-done | bytes 262176 | tf_op jit(solution)/shard_map/all_to_all | solution.py:61
  36.3 0.5 broadcast.224
  36.9 1.2 %reduce.14 = f32[64,1024]{1,0:T(8,128)S(1)} reduce(f32[64,1,1024]{2,1,0:T(1,128)S(1)} %all-to-all-done, f32[]{:T(128)} %broadcast.224), dimensions={1}, to_apply=%all_to_all.23.reduce_sub_computation | reduce | bytes 524292 | tf_op jit(solution)/shard_map/all_to_all | solution.py:61
  38.1 0.1 reshape.251
  38.2 0.2 bitcast_reduce_fusion.4
  38.4 0.1 bitcast_reduce_fusion
  38.7 0.2 reduce_sum.122
  38.9 0.3 reduce_sum.123
  39.3 0.6 reduce_sum.124
  40.0 0.2 broadcast_in_dim.179
  40.2 0.1 broadcast_in_dim.177
  40.3 0.3 fusion.30
  40.6 1.0 reshape.252
  41.7 5.9 %all-to-all-start.1 = ((f32[64,1,1024]{2,1,0:T(1,128)}), f32[64,1,1024]{2,1,0:T(1,128)S(1)}, u32[]{:S(2)}, u32[]{:S(2)}) async-start(f32[64,1,1024]{2,1,0:T(1,128)} %reshape.252), calls=%async_computation.1 | async-start | bytes 524288 | tf_op jit(solution)/shard_map/all_to_all | solution.py:68
  47.6 0.0 copy-start.4
  47.6 5.3 %slice.140 = f32[8,32,16,240]{3,2,1,0:T(8,128)} slice(f32[8,32,16,256]{3,2,1,0:T(8,128)} %copy-done.2), slice={[0:8], [0:32], [0:16], [8:248]} | slice | bytes 7864320 | tf_op jit(solution)/shard_map/slice | solution.py:73
  52.9 7.1 %all-to-all-done.1 = f32[64,1,1024]{2,1,0:T(1,128)S(1)} async-done(((f32[64,1,1024]{2,1,0:T(1,128)}), f32[64,1,1024]{2,1,0:T(1,128)S(1)}, u32[]{:S(2)}, u32[]{:S(2)}) %all-to-all-start.1) | async-done | bytes 262176 | tf_op jit(solution)/shard_map/all_to_all | solution.py:68
  60.0 1.2 %reduce.15 = f32[64,1024]{1,0:T(8,128)S(1)} reduce(f32[64,1,1024]{2,1,0:T(1,128)S(1)} %all-to-all-done.1, f32[]{:T(128)} %broadcast.224), dimensions={1}, to_apply=%all_to_all.25.reduce_sub_computation | reduce | bytes 524292 | tf_op jit(solution)/shard_map/all_to_all | solution.py:68
  61.2 0.1 reshape.253
  61.3 0.2 copy.39
  61.5 0.5 reshape.248
  62.0 0.8 fusion.33
  62.7 1.2 %copy.40 = f32[8,32,16,8]{3,2,1,0:T(8,128)S(1)} copy(f32[8,32,16,8]{3,1,0,2:T(8,128)S(1)} %get-tuple-element.13) | data formatting | bytes 262144 | tf_op jit(solution)/shard_map/slice | solution.py:72
  64.0 1.2 %copy.41 = f32[8,32,16,8]{3,2,1,0:T(8,128)S(1)} copy(f32[8,32,16,8]{3,1,0,2:T(8,128)S(1)} %get-tuple-element.14) | data formatting | bytes 262144 | tf_op jit(solution)/shard_map/slice | solution.py:74
  65.2 1.0 copy-done
  66.1 0.1 maximum_bitcast_fusion.2
  66.2 0.2 maximum_bitcast_fusion.1
  66.4 1.1 pad_maximum_fusion.7
  67.5 1.7 %pad_maximum_fusion = f32[8,32,16,256]{3,2,1,0:T(8,128)S(1)} fusion(f32[8,32,16,8]{3,2,1,0:T(8,128)S(1)} %copy.41, f32[8,32,16,240]{3,2,1,0:T(8,128)S(1)} %copy-done, f32[8,32,16,8]{3,2,1,0:T(8,128)S(1)} %copy.40), kind=kLoop, calls=%fused_computation.4 | loop fusion | flops 2097152 | bytes 8388608 | tf_op jit(solution)/shard_map/concatenate | solution.py:70
  69.2 0.0 copy-start.1
  69.2 5.4 %collective-permute-start.4 = (f32[1,16,256]{2,1,0:T(8,128)S(1)}, f32[1,16,256]{2,1,0:T(8,128)S(1)}, u32[]{:S(2)}, u32[]{:S(2)}) collective-permute-start(f32[1,16,256]{2,1,0:T(8,128)S(1)} %maximum_bitcast_fusion.2), channel_id=1, source_target_pairs={{64,0},{128,64},{192,128},{65,1},{129,65},{193,129},{66,2},{130,66... | collective-permute-start | bytes 49160 | tf_op jit(solution)/shard_map/ppermute | solution.py:29
  74.6 1.3 %collective-permute-start.5 = (f32[32,1,256]{2,1,0:T(1,128)S(1)}, f32[32,1,256]{2,1,0:T(1,128)S(1)}, u32[]{:S(2)}, u32[]{:S(2)}) collective-permute-start(f32[32,1,256]{2,1,0:T(1,128)S(1)} %maximum_bitcast_fusion.1), channel_id=1, source_target_pairs={{1,0},{2,1},{3,2},{4,3},{5,4},{6,5},{7,6},{8,7},{9,8},{10,9},{11,1... | collective-permute-start | bytes 98312 | tf_op jit(solution)/shard_map/ppermute | solution.py:35
  75.9 0.2 pad_maximum_fusion.9
  76.2 1.3 %slice.157 = f32[3,32,16,256]{3,2,1,0:T(8,128)} slice(f32[8,32,16,256]{3,2,1,0:T(8,128)S(1)} %pad_maximum_fusion), slice={[5:8], [0:32], [0:16], [0:256]} | slice | bytes 3145728 | tf_op jit(solution)/shard_map/slice | solution.py:95
  77.4 2.6 %collective-permute-start = (f32[5,2,16,256]{3,2,1,0:T(8,128)S(1)}, f32[5,2,16,256]{3,2,1,0:T(8,128)S(1)}, u32[]{:S(2)}, u32[]{:S(2)}) collective-permute-start(f32[5,2,16,256]{3,2,1,0:T(8,128)S(1)} %get-tuple-element.6), channel_id=1, source_target_pairs={{0,64},{64,128},{128,192},{1,65},{65,129},{129,193},{2,66},{66,130... | collective-permute-start | bytes 491528 | tf_op jit(solution)/shard_map/ppermute | solution.py:17
  80.1 1.9 %collective-permute-start.1 = (f32[5,2,16,256]{3,2,1,0:T(8,128)S(1)}, f32[5,2,16,256]{3,2,1,0:T(8,128)}, u32[]{:S(2)}, u32[]{:S(2)}) collective-permute-start(f32[5,2,16,256]{3,2,1,0:T(8,128)S(1)} %get-tuple-element.7), channel_id=1, source_target_pairs={{64,0},{128,64},{192,128},{65,1},{129,65},{193,129},{66,2},{130,66... | collective-permute-start | bytes 491528 | tf_op jit(solution)/shard_map/ppermute | solution.py:19
  82.1 1.4 %collective-permute-start.3 = (f32[5,32,2,256]{3,1,2,0:T(8,128)S(1)}, f32[5,32,2,256]{3,1,2,0:T(8,128)S(1)}, u32[]{:S(2)}, u32[]{:S(2)}) collective-permute-start(f32[5,32,2,256]{3,1,2,0:T(8,128)S(1)} %copy.44), channel_id=1, source_target_pairs={{1,0},{2,1},{3,2},{4,3},{5,4},{6,5},{7,6},{8,7},{9,8},{10,9},{11,1... | collective-permute-start | bytes 983048 | tf_op jit(solution)/shard_map/ppermute | solution.py:19
  83.4 0.0 collective-permute-done.4
  83.4 0.2 collective-permute-start.2
  83.6 0.3 slice_add_fusion.1
  83.9 0.2 slice.154
  84.1 0.1 add_bitcast_fusion
  84.2 0.0 slice-start
  84.2 0.2 maximum_multiply_fusion
  84.4 7.1 %collective-permute-done.3 = f32[5,32,2,256]{3,1,2,0:T(8,128)S(1)} collective-permute-done((f32[5,32,2,256]{3,1,2,0:T(8,128)S(1)}, f32[5,32,2,256]{3,1,2,0:T(8,128)S(1)}, u32[]{:S(2)}, u32[]{:S(2)}) %collective-permute-start.3) | collective-permute-done | bytes 327712 | tf_op jit(solution)/shard_map/ppermute | solution.py:19
  91.5 0.3 copy.45
  91.8 6.1 %collective-permute-done.2 = f32[5,32,2,256]{3,1,2,0:T(8,128)S(1)} collective-permute-done((f32[5,32,2,256]{3,1,2,0:T(8,128)S(1)}, f32[5,32,2,256]{3,1,2,0:T(8,128)S(1)}, u32[]{:S(2)}, u32[]{:S(2)}) %collective-permute-start.2) | collective-permute-done | bytes 327712 | tf_op jit(solution)/shard_map/ppermute | solution.py:17
  97.9 0.3 copy.43
  98.2 6.1 %fusion.8 = f32[5,32,16,256]{3,2,1,0:T(8,128)} fusion(f32[5,32,16,256]{3,2,1,0:T(8,128)S(1)} %slice-done, f32[5,2,16,256]{3,2,1,0:T(8,128)} %collective-permute-done.1, f32[5,2,16,256]{3,2,1,0:T(8,128)S(1)} %collective-permute-done, f32[5,32,2,256]{3,2,1,0:T(2,128)S(1)} %copy.45, f32[5,32,2,256]{3,2,1,0:T(2,128)S(1)} %copy.43, ...), kind=kLoop, calls=%fused_computation.22 | loop fusion | flops 18350080 | bytes 6231040 | tf_op jit(solution)/shard_map/add | solution.py:89
  104.3 4.2 %pad_maximum_fusion.1 = f32[8,32,16,256]{3,2,1,0:T(8,128)} fusion(f32[3,32,16,256]{3,2,1,0:T(8,128)S(1)} %maximum_multiply_fusion, f32[5,32,16,256]{3,2,1,0:T(8,128)} %fusion.8), kind=kLoop, calls=%fused_computation.5 | loop fusion | flops 1048576 | bytes 8388608 | tf_op jit(solution)/shard_map/concatenate | solution.py:95
  (37 shorter events, 0.4 us)
Async XLA Ops:
  0.6 2.2 %copy-start.3 = (f32[3,32,16,256]{3,2,1,0:T(8,128)S(1)}, f32[3,32,16,256]{3,2,1,0:T(8,128)}, u32[]{:S(2)}) copy-start(f32[3,32,16,256]{3,2,1,0:T(8,128)} %param.5) | copy-start | bytes 4718596
  2.9 2.0 %copy-start.2 = (f32[8,32,16,256]{3,2,1,0:T(8,128)}, f32[8,32,16,256]{3,2,1,0:T(8,128)S(1)}, u32[]{:S(2)}) copy-start(f32[8,32,16,256]{3,2,1,0:T(8,128)S(1)} %constant_dynamic-update-slice_fusion) | copy-start | bytes 12582916
  6.3 17.0 %copy-start.5 = (s32[16]{0:T(128)S(1)}, s32[16]{0:T(128)}, u32[]{:S(2)}) copy-start(s32[16]{0:T(128)} %param.6) | copy-start | bytes 196
  8.1 28.2 %all-to-all-start = ((f32[64,1,1024]{2,1,0:T(1,128)}), f32[64,1,1024]{2,1,0:T(1,128)S(1)}, u32[]{:S(2)}, u32[]{:S(2)}) async-start(f32[64,1,1024]{2,1,0:T(1,128)} %reshape.250), calls=%async_computation | async-start | bytes 524288 | tf_op jit(solution)/shard_map/all_to_all | solution.py:61
  41.7 18.3 %all-to-all-start.1 = ((f32[64,1,1024]{2,1,0:T(1,128)}), f32[64,1,1024]{2,1,0:T(1,128)S(1)}, u32[]{:S(2)}, u32[]{:S(2)}) async-start(f32[64,1,1024]{2,1,0:T(1,128)} %reshape.252), calls=%async_computation.1 | async-start | bytes 524288 | tf_op jit(solution)/shard_map/all_to_all | solution.py:68
  47.6 5.3 %copy-start.4 = (f32[5,256]{1,0:T(8,128)S(1)}, f32[5,256]{1,0:T(8,128)}, u32[]{:S(2)}) copy-start(f32[5,256]{1,0:T(8,128)} %param.7) | copy-start | bytes 15364
  64.0 2.2 %copy-start = (f32[8,32,16,240]{3,2,1,0:T(8,128)S(1)}, f32[8,32,16,240]{3,2,1,0:T(8,128)}, u32[]{:S(2)}) copy-start(f32[8,32,16,240]{3,2,1,0:T(8,128)} %slice.140) | copy-start | bytes 11796484
  69.2 15.0 %copy-start.1 = (f32[8,32,16,256]{3,2,1,0:T(8,128)}, f32[8,32,16,256]{3,2,1,0:T(8,128)S(1)}, u32[]{:S(2)}) copy-start(f32[8,32,16,256]{3,2,1,0:T(8,128)S(1)} %pad_maximum_fusion) | copy-start | bytes 12582916
  69.2 14.2 %collective-permute-start.4 = (f32[1,16,256]{2,1,0:T(8,128)S(1)}, f32[1,16,256]{2,1,0:T(8,128)S(1)}, u32[]{:S(2)}, u32[]{:S(2)}) collective-permute-start(f32[1,16,256]{2,1,0:T(8,128)S(1)} %maximum_bitcast_fusion.2), channel_id=1, source_target_pairs={{64,0},{128,64},{192,128},{65,1},{129,65},{193,129},{66,2},{130,66... | collective-permute-start | bytes 49160 | tf_op jit(solution)/shard_map/ppermute | solution.py:29
  74.6 9.0 %collective-permute-start.5 = (f32[32,1,256]{2,1,0:T(1,128)S(1)}, f32[32,1,256]{2,1,0:T(1,128)S(1)}, u32[]{:S(2)}, u32[]{:S(2)}) collective-permute-start(f32[32,1,256]{2,1,0:T(1,128)S(1)} %maximum_bitcast_fusion.1), channel_id=1, source_target_pairs={{1,0},{2,1},{3,2},{4,3},{5,4},{6,5},{7,6},{8,7},{9,8},{10,9},{11,1... | collective-permute-start | bytes 98312 | tf_op jit(solution)/shard_map/ppermute | solution.py:35
  77.4 20.7 %collective-permute-start = (f32[5,2,16,256]{3,2,1,0:T(8,128)S(1)}, f32[5,2,16,256]{3,2,1,0:T(8,128)S(1)}, u32[]{:S(2)}, u32[]{:S(2)}) collective-permute-start(f32[5,2,16,256]{3,2,1,0:T(8,128)S(1)} %get-tuple-element.6), channel_id=1, source_target_pairs={{0,64},{64,128},{128,192},{1,65},{65,129},{129,193},{2,66},{66,130... | collective-permute-start | bytes 491528 | tf_op jit(solution)/shard_map/ppermute | solution.py:17
  80.1 18.1 %collective-permute-start.1 = (f32[5,2,16,256]{3,2,1,0:T(8,128)S(1)}, f32[5,2,16,256]{3,2,1,0:T(8,128)}, u32[]{:S(2)}, u32[]{:S(2)}) collective-permute-start(f32[5,2,16,256]{3,2,1,0:T(8,128)S(1)} %get-tuple-element.7), channel_id=1, source_target_pairs={{64,0},{128,64},{192,128},{65,1},{129,65},{193,129},{66,2},{130,66... | collective-permute-start | bytes 491528 | tf_op jit(solution)/shard_map/ppermute | solution.py:19
  82.1 9.4 %collective-permute-start.3 = (f32[5,32,2,256]{3,1,2,0:T(8,128)S(1)}, f32[5,32,2,256]{3,1,2,0:T(8,128)S(1)}, u32[]{:S(2)}, u32[]{:S(2)}) collective-permute-start(f32[5,32,2,256]{3,1,2,0:T(8,128)S(1)} %copy.44), channel_id=1, source_target_pairs={{1,0},{2,1},{3,2},{4,3},{5,4},{6,5},{7,6},{8,7},{9,8},{10,9},{11,1... | collective-permute-start | bytes 983048 | tf_op jit(solution)/shard_map/ppermute | solution.py:19
  83.4 14.5 %collective-permute-start.2 = (f32[5,32,2,256]{3,1,2,0:T(8,128)S(1)}, f32[5,32,2,256]{3,1,2,0:T(8,128)S(1)}, u32[]{:S(2)}, u32[]{:S(2)}) collective-permute-start(f32[5,32,2,256]{3,1,2,0:T(8,128)S(1)} %copy.42), channel_id=1, source_target_pairs={{0,1},{1,2},{2,3},{3,4},{4,5},{5,6},{6,7},{7,8},{8,9},{9,10},{10,1... | collective-permute-start | bytes 983048 | tf_op jit(solution)/shard_map/ppermute | solution.py:17
  84.2 13.9 %slice-start = ((f32[8,32,16,256]{3,2,1,0:T(8,128)}), f32[5,32,16,256]{3,2,1,0:T(8,128)S(1)}, s32[]{:S(2)}) async-start(f32[8,32,16,256]{3,2,1,0:T(8,128)} %copy-done.1), calls=%async_computation.2 | async-start | bytes 5242880 | tf_op jit(solution)/shard_map/slice | solution.py:78
where the time goes:
time: 109 us; the launch traced here: 108 us
  starting transfers between devices  33.8 us (31%)
  waiting for transfers between devices  33.3 us (31%)
  local copies, waits for them, and re-layouts  21.1 us (19%)
  other arithmetic  19.1 us (18%)
  between operations  1.15 us (1%)
    all_to_all x1, starting transfers between devices, body(): whole = lax.all_to_all(slab, 'phi', split_axis=1, concat_axis=0, tiled=True)  15.1 us
    all_to_all x1, waiting for transfers between devices, body(): whole = lax.all_to_all(slab, 'phi', split_axis=1, concat_axis=0, tiled=True)  13 us
    ppermute x2, waiting for transfers between devices, extended(): lax.ppermute(head, axis, [((i + 1) % count, i) for i in range(ends)])  7.09 us
    all_to_all x1, waiting for transfers between devices, body(): back = lax.all_to_all(means, 'phi', split_axis=0, concat_axis=1, tiled=True)  7.07 us
    unnamed x17, local copies, waits for them, and re-layouts  6.77 us
    ppermute x2, waiting for transfers between devices, extended(): lax.ppermute(tail, axis, [(i, (i + 1) % count) for i in range(ends)])  6.13 us
    add x1, other arithmetic, body(): smoothed = hydro + diffusion[:, None, None, :] * change  6.09 us
    all_to_all x1, starting transfers between devices, body(): back = lax.all_to_all(means, 'phi', split_axis=0, concat_axis=1, tiled=True)  5.93 us
  transfers between devices with their start and end apart: 8, of which 4 were waited for; matrix products, arithmetic and copies ran while one was open for 8% of the time, Pallas kernels for 0%

commit v1 on v0

v1 whole, which is shorter than its diff:
```python
import jax
import jax.numpy as jnp
from jax import lax
from jax.experimental import pallas as pl
from jax.experimental.pallas import tpu as pltpu
from jax.sharding import PartitionSpec as P

F32 = jnp.float32
MESH = pl.DeviceIdType.MESH
NV, NF, FIELDS = 5, 3, 8
ROWS, CELLS, THETA = 32, 16, 256
NZ, NG, NROW = 8, 8, 4
EARLY = 2
FAR_FIRST = (4, 3, 5, 2, 6, 1, 7)


def lanes(shape):
    return lax.broadcasted_iota(jnp.int32, shape, len(shape) - 1)


def sublanes(shape):
    return lax.broadcasted_iota(jnp.int32, shape, len(shape) - 2)


def exchange(
    widths, hydro, face, halo, radial, polar,
    hv, fv, la, zsum, gsum, edge, first, last, first_in, last_in, la_in,
    load_sem, q_send, q_recv, qn_send, qn_recv, qp_send, qp_recv,
    la_send, la_recv, e_send, e_recv, g_send, g_recv,
    p_send, p_recv, r_send, r_recv,
):
    row, phi = lax.axis_index("row"), lax.axis_index("phi")
    z, g = phi % NZ, phi // NZ
    nphi = NZ * NG
    after, before = (phi + 1) % nphi, (phi + nphi - 1) % nphi
    has_prev, has_next = row > 0, row < NROW - 1

    def peer(d):
        return g * NZ + (z + d) % NZ

    def group(d):
        return ((g + d) % NG) * NZ + z

    loads = [pltpu.make_async_copy(hydro.at[i], hv.at[i], load_sem.at[i]) for i in range(NV)]
    loads += [pltpu.make_async_copy(face.at[i], fv.at[i], load_sem.at[NV + i]) for i in range(NF)]
    for copy in loads:
        copy.start()

    zsum[:, ROWS:, :] = jnp.zeros((NZ, 8, 128), F32)
    barrier = pltpu.get_barrier_semaphore()

    def hello(r, p):
        pl.semaphore_signal(barrier, inc=1, device_id=(r, p), device_id_type=MESH)

    for d in range(1, NZ):
        hello(row, peer(d))
        hello(row, group(d))

    @pl.when(has_prev)
    def _():
        for d in range(NZ):
            hello(row - 1, peer(d))

    @pl.when(has_next)
    def _():
        for d in range(NZ):
            hello(row + 1, peer(d))

    @pl.when(z == 0)
    def _():
        hello(row, before)

    @pl.when(z == NZ - 1)
    def _():
        hello(row, after)

    lane = lanes((8, 128))
    sub = sublanes((8, 128))
    width = jnp.zeros((8, 128), jnp.int32)
    for c in range(16):
        width = jnp.where(lane % 16 == c, widths[(c + 8) % 16], width)
    low = lane < 64

    for copy in loads:
        copy.wait()

    def pack(block, carry):
        q8 = jnp.zeros((8, 128), F32)
        f8 = jnp.zeros((8, 128), F32)
        l8 = jnp.zeros((8, 128), F32)
        for i in range(8):
            r = block * 8 + i
            parts = []
            for j in range(2):
                packed = None
                for f in range(FIELDS):
                    ref, k = (hv, f) if f < NV else (fv, f - NV)
                    t0 = ref[k, r, 8 * j:8 * j + 8, 0:128]
                    t1 = ref[k, r, 8 * j:8 * j + 8, 128:256]
                    t = pltpu.roll(jnp.where(low, t0, t1), (8 + 16 * f) % 128, 1)
                    packed = t if packed is None else jnp.where(lane // 16 == f, t, packed)
                parts.append(packed)
            sums, local = [], []
            for p in parts:
                s2 = p + jnp.where(sub % 2 == 0, pltpu.roll(p, 7, 0), pltpu.roll(p, 1, 0))
                s4 = s2 + jnp.where(sub % 4 < 2, pltpu.roll(s2, 6, 0), pltpu.roll(s2, 2, 0))
                s8 = s4 + pltpu.roll(s4, 4, 0)
                sums.append(s8)
                local.append((s2, s4, s8))
            s16 = sums[0] + sums[1]
            for j, (s2, s4, s8) in enumerate(local):
                mean = jnp.where(width == 2, s2 * 0.5, s16 * 0.0625)
                mean = jnp.where(width == 4, s4 * 0.25, mean)
                mean = jnp.where(width == 8, s8 * 0.125, mean)
                la[r, 8 * j:8 * j + 8, :] = mean
                local[j] = mean
            q8 = jnp.where(sub == i, s16, q8)
            f8 = jnp.where(sub == i, pltpu.roll(local[0], i, 0) if i else local[0], f8)
            l8 = jnp.where(sub == i, pltpu.roll(local[1], (i + 1) % 8, 0) if i < 7 else local[1], l8)
        at = pl.ds(pl.multiple_of(block * 8, 8), 8)
        zsum[z, at, :] = q8
        first[at, :] = f8
        last[at, :] = l8
        return carry

    lax.fori_loop(0, ROWS // 8, pack, 0)

    hellos = 2 * (NZ - 1) + NZ * (has_prev.astype(jnp.int32) + has_next.astype(jnp.int32))
    hellos += (z == 0).astype(jnp.int32) + (z == NZ - 1).astype(jnp.int32)
    pl.semaphore_wait(barrier, hellos)

    def remote(src, dst, ssem, rsem, r, p):
        return pltpu.make_async_remote_copy(
            src_ref=src, dst_ref=dst, send_sem=ssem, recv_sem=rsem,
            device_id=(r, p), device_id_type=MESH,
        )

    def q_copy(d):
        ref = zsum.at[z, 0:ROWS, :]
        return remote(ref, ref, q_send.at[d], q_recv.at[d], row, peer(d))

    def q_down(d):
        return remote(
            zsum.at[z, 0:2, :], zsum.at[z, ROWS + 2:ROWS + 4, :],
            qn_send.at[d], qn_recv.at[d], row - 1, peer(d),
        )

    def q_up(d):
        return remote(
            zsum.at[z, ROWS - 2:ROWS, :], zsum.at[z, ROWS:ROWS + 2, :],
            qp_send.at[d], qp_recv.at[d], row + 1, peer(d),
        )

    for d in FAR_FIRST:
        q_copy(d).start()

    @pl.when(has_prev)
    def _():
        for d in FAR_FIRST + (0,):
            q_down(d).start()

    @pl.when(has_next)
    def _():
        for d in FAR_FIRST + (0,):
            q_up(d).start()

    edge_first = remote(first, first_in, la_send.at[0], la_recv.at[0], row, before)
    edge_last = remote(last, last_in, la_send.at[1], la_recv.at[1], row, after)
    edge_first.start()
    edge_last.start()
    la_down = remote(la.at[0:2], la_in.at[2:4], la_send.at[2], la_recv.at[2], row - 1, phi)
    la_up = remote(la.at[ROWS - 2:ROWS], la_in.at[0:2], la_send.at[3], la_recv.at[3], row + 1, phi)

    down = [remote(hv.at[:, 0:2], radial.at[0:NV, 2:4], r_send.at[0], r_recv.at[0], row - 1, phi)]
    down += [remote(fv.at[0, 0:1], radial.at[NV, 2:3], r_send.at[1], r_recv.at[1], row - 1, phi)]
    up = [remote(hv.at[:, ROWS - 2:ROWS], radial.at[0:NV, 0:2], r_send.at[2], r_recv.at[2], row + 1, phi)]

    @pl.when(has_prev)
    def _():
        la_down.start()
        for copy in down:
            copy.start()

    @pl.when(has_next)
    def _():
        la_up.start()
        for copy in up:
            copy.start()

    bulk = []
    for i in range(NV):
        bulk.append(remote(
            hv.at[i, :, CELLS - 2:CELLS, :], halo.at[i, :, 6:8, :],
            p_send.at[2 * i], p_recv.at[2 * i], row, after,
        ))
        bulk.append(remote(
            hv.at[i, :, 0:2, :], halo.at[i, :, 0:2, :],
            p_send.at[2 * i + 1], p_recv.at[2 * i + 1], row, before,
        ))
    bulk.append(remote(
        fv.at[2, :, 0:1, :], halo.at[NV, :, 0:1, :],
        p_send.at[2 * NV], p_recv.at[2 * NV], row, before,
    ))
    for copy in bulk[:2 * EARLY]:
        copy.start()

    for d in FAR_FIRST:
        q_copy(d).wait_recv()

    @pl.when(has_prev)
    def _():
        for d in FAR_FIRST + (0,):
            q_up(d).wait_recv()

    @pl.when(has_next)
    def _():
        for d in FAR_FIRST + (0,):
            q_down(d).wait_recv()

    def z_sums(at):
        pair, quad = (at // 2) * 2, (at // 4) * 4
        s32 = zsum[pair] + zsum[pair + 1]
        s64 = (zsum[quad] + zsum[quad + 1]) + (zsum[quad + 2] + zsum[quad + 3])
        return s32, s64

    tall = (ROWS + 8, 128)
    width = jnp.broadcast_to(width[0:1], tall)
    total = zsum[0]
    for i in range(1, NZ):
        total = total + zsum[i]
    gsum[g] = total

    def g_copy(d):
        return remote(gsum.at[g], gsum.at[g], g_send.at[d], g_recv.at[d], row, group(d))

    for d in (5, 3, 7, 1, 6, 2, 4):
        g_copy(d).start()

    s32, s64 = z_sums(z)
    small = jnp.where(width == 32, s32 * (1 / 32), s64 * (1 / 64))
    s32p, s64p = z_sums((z + NZ - 1) % NZ)
    s32n, s64n = z_sums((z + 1) % NZ)
    edge[0] = jnp.where(width == 32, s32p * (1 / 32), s64p * (1 / 64))[:ROWS]
    edge[1] = jnp.where(width == 32, s32n * (1 / 32), s64n * (1 / 64))[:ROWS]
    edge_up = remote(edge.at[0], edge.at[2], e_send.at[0], e_recv.at[0], row, group(1))
    edge_down = remote(edge.at[1], edge.at[3], e_send.at[1], e_recv.at[1], row, group(NG - 1))

    edge_up.start()
    edge_down.start()

    for copy in bulk[2 * EARLY:]:
        copy.start()

    for d in (5, 3, 7, 1, 6, 2, 4):
        g_copy(d).wait_recv()
    edge_up.wait_recv()
    edge_down.wait_recv()
    edge_first.wait_recv()
    edge_last.wait_recv()

    def g_means(at, small):
        pair, quad = (at // 2) * 2, (at // 4) * 4
        mean = jnp.where(width == 128, gsum[at] * (1 / 128), small)
        mean = jnp.where(width == 256, (gsum[pair] + gsum[pair + 1]) * (1 / 256), mean)
        four = (gsum[quad] + gsum[quad + 1]) + (gsum[quad + 2] + gsum[quad + 3])
        mean = jnp.where(width == 512, four * (1 / 512), mean)
        whole = gsum[0]
        for i in range(1, NG):
            whole = whole + gsum[i]
        return jnp.where(width == 1024, whole * (1 / 1024), mean)

    mean = g_means(g, small)
    gp = jnp.where(z == 0, (g + NG - 1) % NG, g)
    gn = jnp.where(z == NZ - 1, (g + 1) % NG, g)
    pad = jnp.zeros((8, 128), F32)
    ep = jnp.concatenate([jnp.where(z == 0, edge[2], edge[0]), pad])
    en = jnp.concatenate([jnp.where(z == NZ - 1, edge[3], edge[1]), pad])
    mean_p = jnp.where(width <= 16, jnp.concatenate([last_in[...], pad]), g_means(gp, ep))
    mean_n = jnp.where(width <= 16, jnp.concatenate([first_in[...], pad]), g_means(gn, en))
    narrow = jnp.broadcast_to(width[0:1], (CELLS, 128)) <= 16
    for r in range(ROWS):
        polar[r, 0:CELLS, :] = jnp.where(narrow, la[r], mean[r:r + 1])
        polar[r, CELLS:, :] = jnp.where(sub < 4, mean_n[r:r + 1], mean_p[r:r + 1])

    @pl.when(has_prev)
    def _():
        la_up.wait_recv()

    @pl.when(has_next)
    def _():
        la_down.wait_recv()

    for i in range(4):
        r = ROWS + i
        polar[r, 0:CELLS, :] = jnp.where(narrow, la_in[i], mean[r:r + 1])
        polar[r, CELLS:, :] = jnp.zeros((8, 128), F32)

    for copy in bulk:
        copy.wait_recv()

    @pl.when(has_prev)
    def _():
        for copy in up:
            copy.wait_recv()

    @pl.when(has_next)
    def _():
        for copy in down:
            copy.wait_recv()

    for d in FAR_FIRST:
        q_copy(d).wait_send()
        g_copy(d).wait_send()
    for copy in bulk + [edge_up, edge_down, edge_first, edge_last]:
        copy.wait_send()

    @pl.when(has_prev)
    def _():
        la_down.wait_send()
        for copy in down:
            copy.wait_send()
        for d in range(NZ):
            q_down(d).wait_send()

    @pl.when(has_next)
    def _():
        la_up.wait_send()
        for copy in up:
            copy.wait_send()
        for d in range(NZ):
            q_up(d).wait_send()


def run_exchange(widths, hydro, face):
    dma = pltpu.SemaphoreType.DMA
    return pl.pallas_call(
        exchange,
        out_shape=(
            jax.ShapeDtypeStruct((NV + 1, ROWS, 8, THETA), F32),
            jax.ShapeDtypeStruct((NV + 1, 4, CELLS, THETA), F32),
            jax.ShapeDtypeStruct((ROWS + 4, CELLS + 8, 128), F32),
        ),
        in_specs=[
            pl.BlockSpec(memory_space=pltpu.SMEM),
            pl.BlockSpec(memory_space=pl.ANY),
            pl.BlockSpec(memory_space=pl.ANY),
        ],
        out_specs=(
            pl.BlockSpec(memory_space=pl.ANY),
            pl.BlockSpec(memory_space=pl.ANY),
            pl.BlockSpec(memory_space=pltpu.VMEM),
        ),
        scratch_shapes=[
            pltpu.VMEM((NV, ROWS, CELLS, THETA), F32),
            pltpu.VMEM((NF, ROWS, CELLS, THETA), F32),
            pltpu.VMEM((ROWS, CELLS, 128), F32),
            pltpu.VMEM((NZ, ROWS + 8, 128), F32),
            pltpu.VMEM((NG, ROWS + 8, 128), F32),
            pltpu.VMEM((4, ROWS, 128), F32),
            pltpu.VMEM((ROWS, 128), F32),
            pltpu.VMEM((ROWS, 128), F32),
            pltpu.VMEM((ROWS, 128), F32),
            pltpu.VMEM((ROWS, 128), F32),
            pltpu.VMEM((4, CELLS, 128), F32),
            dma((FIELDS,)),
            dma((NZ,)), dma((NZ,)), dma((NZ,)), dma((NZ,)), dma((NZ,)), dma((NZ,)),
            dma((4,)), dma((4,)), dma((2,)), dma((2,)), dma((NG,)), dma((NG,)),
            dma((2 * NV + 1,)), dma((2 * NV + 1,)), dma((3,)), dma((3,)),
        ],
        compiler_params=pltpu.CompilerParams(collective_id=0, has_side_effects=True),
        name="exchange",
    )(widths, hydro, face)


def update(hydro, face, halo, radial, polar, diffusion, conserved, faces_out, s, band):
    f = pl.program_id(0)
    row = lax.axis_index("row")
    shift = (120 - 16 * f) % 128
    lane = lanes((8, 128))
    sub = sublanes((8, 128))
    left, right = lane < 8, lane >= 120

    def merged(raw0, raw1, packed):
        p = pltpu.roll(packed, shift, 1)
        return jnp.where(left, p, raw0), jnp.where(right, p, raw1)

    def put(r, at, raw, packed):
        a, b = merged(raw[:, 0:128], raw[:, 128:256], packed)
        s[r, at:at + 8, 0:128] = a
        s[r, at:at + 8, 128:256] = b

    def edge_row(i):
        r = ROWS + 2 + (i - 2) if i >= 2 else i
        for j in (0, 8):
            put(r, j, radial[0, i, j:j + 8, :], polar[ROWS + i, j:j + 8, :])

    def clear_row(i):
        r = ROWS + 2 + (i - 2) if i >= 2 else i
        s[r] = jnp.zeros((CELLS + 8, THETA), F32)

    @pl.when(f == 0)
    def _():
        i0 = lax.broadcasted_iota(jnp.int32, (THETA, THETA), 0)
        i1 = lax.broadcasted_iota(jnp.int32, (THETA, THETA), 1)
        apart = jnp.abs(i0 - i1)
        band[...] = jnp.where(apart == 1, 16.0, jnp.where(apart == 2, -1.0, 0.0)).astype(jnp.bfloat16)

    @pl.when(row > 0)
    def _():
        edge_row(0)
        edge_row(1)

    @pl.when(row == 0)
    def _():
        clear_row(0)
        clear_row(1)

    @pl.when(row < NROW - 1)
    def _():
        edge_row(2)
        edge_row(3)

    @pl.when(row == NROW - 1)
    def _():
        clear_row(2)
        clear_row(3)

    def fill(ref):
        def step(r, carry):
            for j in (0, 8):
                put(r + 2, j, ref[0, r, j:j + 8, :], polar[r, j:j + 8, :])
            put(r + 2, 16, halo[0, r], polar[r, 16:24, :])
            return carry
        lax.fori_loop(0, ROWS, step, 0, unroll=4)

    def around(t0, t1, h, k):
        if k > 0:
            edge = sub >= 8 - k
            a, b, c = (pltpu.roll(t, 8 - k, 0) for t in (t0, t1, h))
            return jnp.where(edge, b, a), jnp.where(edge, c, b)
        edge = sub < -k
        a, b, c = (pltpu.roll(t, -k, 0) for t in (t0, t1, h))
        return jnp.where(edge, c, a), jnp.where(edge, a, b)

    @pl.when(f < NV)
    def _():
        fill(hydro)
        diff = diffusion[pl.ds(f, 1), :] * (1.0 / 12.0)
        batch = 4

        def step(block, carry):
            r0 = block * batch
            centre = jnp.concatenate([s[r0 + i + 2, 0:CELLS, :] for i in range(batch)], 0)
            high = centre.astype(jnp.bfloat16)
            rest = (centre - high.astype(F32)).astype(jnp.bfloat16)
            theta = jnp.dot(high, band[...], preferred_element_type=F32)
            theta = theta + jnp.dot(rest, band[...], preferred_element_type=F32)
            for i in range(batch):
                r = r0 + i + 2
                for half in range(2):
                    ln = slice(128 * half, 128 * half + 128)
                    t = [s[r, 8 * j:8 * j + 8, ln] for j in range(3)]
                    n1, n2 = around(*t, 1), around(*t, 2)
                    p1, p2 = around(*t, -1), around(*t, -2)
                    for j in range(2):
                        at = slice(8 * j, 8 * j + 8)
                        near = (n1[j] + p1[j]) + (s[r - 1, at, ln] + s[r + 1, at, ln])
                        far = (n2[j] + p2[j]) + (s[r - 2, at, ln] + s[r + 2, at, ln])
                        change = 16.0 * near - far - 90.0 * t[j]
                        change = change + theta[16 * i + 8 * j:16 * i + 8 * j + 8, ln]
                        conserved[0, r0 + i, at, ln] = t[j] + diff[:, ln] * change
            return carry

        lax.fori_loop(0, ROWS // batch, step, 0)

    @pl.when(f >= NV)
    def _():
        fill(face)

        def copy(r, carry):
            faces_out[0, r] = s[r + 2, 0:CELLS, :]
            return carry
        lax.fori_loop(0, ROWS, copy, 0, unroll=4)

    @pl.when(f == NV)
    def _():
        def step(r, carry):
            conserved[0, r] = 0.5 * (s[r + 2, 0:CELLS, :] + s[r + 3, 0:CELLS, :])
            return carry
        lax.fori_loop(0, ROWS, step, 0, unroll=4)

    @pl.when(f == NV + 1)
    def _():
        def step(r, carry):
            for j in (0, 8):
                a, b = s[r + 2, j:j + 8, 0:128], s[r + 2, j:j + 8, 128:256]
                ra, rb = pltpu.roll(a, 127, 1), pltpu.roll(b, 127, 1)
                conserved[0, r, j:j + 8, 0:128] = 0.5 * (a + jnp.where(lane == 127, rb, ra))
                conserved[0, r, j:j + 8, 128:256] = 0.5 * (b + jnp.where(lane == 127, 0.0, rb))
            return carry
        lax.fori_loop(0, ROWS, step, 0, unroll=4)

    @pl.when(f == NV + 2)
    def _():
        def step(r, carry):
            for half in range(2):
                ln = slice(128 * half, 128 * half + 128)
                t = [s[r + 2, 8 * j:8 * j + 8, ln] for j in range(3)]
                n1 = around(*t, 1)
                for j in range(2):
                    conserved[0, r, 8 * j:8 * j + 8, ln] = 0.5 * (t[j] + n1[j])
            return carry
        lax.fori_loop(0, ROWS, step, 0, unroll=4)


def run_update(hydro, face, halo, radial, polar, diffusion):
    def hyd(f):
        return (jnp.minimum(f, NV - 1), 0, 0, 0)

    def fac(f):
        return (jnp.maximum(f - NV, 0), 0, 0, 0)

    def six(f):
        return (jnp.where(f == NV + 2, NV, jnp.minimum(f, NV)), 0, 0, 0)

    return pl.pallas_call(
        update,
        grid=(FIELDS,),
        out_shape=(
            jax.ShapeDtypeStruct((FIELDS, ROWS, CELLS, THETA), F32),
            jax.ShapeDtypeStruct((NF, ROWS, CELLS, THETA), F32),
        ),
        in_specs=[
            pl.BlockSpec((1, ROWS, CELLS, THETA), hyd),
            pl.BlockSpec((1, ROWS, CELLS, THETA), fac),
            pl.BlockSpec((1, ROWS, 8, THETA), six),
            pl.BlockSpec((1, 4, CELLS, THETA), six),
            pl.BlockSpec((ROWS + 4, CELLS + 8, 128), lambda f: (0, 0, 0)),
            pl.BlockSpec((NV, THETA), lambda f: (0, 0)),
        ],
        out_specs=(
            pl.BlockSpec((1, ROWS, CELLS, THETA), lambda f: (f, 0, 0, 0)),
            pl.BlockSpec((1, ROWS, CELLS, THETA), fac),
        ),
        scratch_shapes=[
            pltpu.VMEM((ROWS + 4, CELLS + 8, THETA), F32),
            pltpu.VMEM((THETA, THETA), jnp.bfloat16),
        ],
        name="update",
    )(hydro, face, halo, radial, polar, diffusion)


def body(hydro, face, widths, diffusion):
    halo, radial, polar = run_exchange(widths, hydro, face)
    return run_update(hydro, face, halo, radial, polar, diffusion)


def solution(mesh):
    spec = P(None, "row", "phi", None)
    return jax.shard_map(
        body, mesh=mesh, in_specs=(spec, spec, P(), P()), out_specs=(spec, spec), check_vma=False
    )
```

time: 109 us -> 49.7 us (0.46)
  Pallas kernels: 0 us -> 48.9 us
  starting transfers between devices: 33.8 us -> 0 us
  waiting for transfers between devices: 33.3 us -> 0 us
  local copies, waits for them, and re-layouts: 21.1 us -> 0 us
  other arithmetic: 19.1 us -> 0 us
    pallas_call x0 -> x2, Pallas kernels: none -> 48.9 us  [the longest x1 31.1 us: run_exchange(): pl.pallas_call(exchange, out_shape=(jax.ShapeDtypeStruct((NV + 1, ROWS, 8...]
    all_to_all x2 -> x0, starting transfers between devices: 21 us -> none  [the longest x1 15.1 us: body(): whole = lax.all_to_all(slab, 'phi', split_axis=1, concat_axis=0, tiled=True)]
    all_to_all x2 -> x0, waiting for transfers between devices: 20.1 us -> none  [the longest x1 13 us: body(): whole = lax.all_to_all(slab, 'phi', split_axis=1, concat_axis=0, tiled=True)]
    ppermute x6 -> x0, waiting for transfers between devices: 13.2 us -> none  [the longest x2 7.09 us: extended(): lax.ppermute(head, axis, [((i + 1) % count, i) for i in range(ends)])]
    ppermute x6 -> x0, starting transfers between devices: 12.8 us -> none  [the longest x1 5.41 us: passed_along(): lax.ppermute(value, axis, [(source, source + steps) for source in range(i...]
    slice x13 -> x0, local copies, waits for them, and re-layouts: 10.7 us -> none  [the longest x1 5.26 us: body(): fields[..., CYCLES:theta_cells - CYCLES]]
    unnamed x17 -> x0, local copies, waits for them, and re-layouts: 6.77 us -> none
    add x2 -> x0, other arithmetic: 6.4 us -> none  [the longest x1 6.09 us: body(): smoothed = hydro + diffusion[:, None, None, :] * change]
  transfers between devices with their start and end apart: 8 -> 0, of which waited for: 4 -> 0; matrix products, arithmetic and copies ran while one was open for 8% -> 0% of each run, Pallas kernels for 0% -> 0%
where the time goes in v1:
time: 49.7 us; the launch traced here: 49.5 us
  Pallas kernels  48.9 us (98%)
  between operations  0.64 us (1%)
    pallas_call x1, Pallas kernels, run_exchange(): pl.pallas_call(exchange, out_shape=(jax.ShapeDtypeStruct((NV + 1, ROWS, 8...  31.1 us
    pallas_call x1, Pallas kernels, run_update(): pl.pallas_call(update, grid=(FIELDS,), out_shape=(jax.ShapeDtypeStruct((F...  17.7 us

profile of v1, /device:TPU:1, one launch (start us, length us, event | category | flops | bytes accessed | tf_op | source)
XLA Modules:
  0.0 49.5 jit_solution(17944245014546074267)
XLA Ops:
  0.6 31.1 %exchange.1 = (f32[6,32,8,256]{3,2,1,0:T(8,128)}, f32[6,4,16,256]{3,2,1,0:T(8,128)}, f32[36,24,128]{2,1,0:T(8,128)}) custom-call(s32[16]{0:T(128)} %widths.1, f32[5,32,16,256]{3,2,1,0:T(8,128)} %hydro.3, f32[3,32,16,256]{3,2,1,0:T(8,128)} %face.3), custom_call_target="tpu_custom_call" | custom-call | tf_op jit(solution)/shard_map/exchange/pallas_call | solution.py:336
  31.8 17.7 %update.1 = (f32[8,32,16,256]{3,2,1,0:T(8,128)}, f32[3,32,16,256]{3,2,1,0:T(8,128)}) custom-call(f32[5,32,16,256]{3,2,1,0:T(8,128)} %hydro.3, f32[3,32,16,256]{3,2,1,0:T(8,128)} %face.3, f32[6,32,8,256]{3,2,1,0:T(8,128)} %get-tuple-element.5.halo, f32[6,4,16,256]{3,2,1,0:T(8,128)} %get-tuple-element.6.radial, f32[36,24,128]{2,1,0:T(8,128)} %get-tuple-element.7.polar, ...), custom_call_target="tpu_custom_call" | custom-call | tf_op jit(solution)/shard_map/update/pallas_call | solution.py:526

commit v2 on v1

--- a/solution.py
+++ b/solution.py
@@ -342,12 +342,12 @@
         ),
         in_specs=[
             pl.BlockSpec(memory_space=pltpu.SMEM),
-            pl.BlockSpec(memory_space=pl.ANY),
-            pl.BlockSpec(memory_space=pl.ANY),
+            pl.BlockSpec(memory_space=pltpu.HBM),
+            pl.BlockSpec(memory_space=pltpu.HBM),
         ],
         out_specs=(
-            pl.BlockSpec(memory_space=pl.ANY),
-            pl.BlockSpec(memory_space=pl.ANY),
+            pl.BlockSpec(memory_space=pltpu.VMEM),
+            pl.BlockSpec(memory_space=pltpu.VMEM),
             pl.BlockSpec(memory_space=pltpu.VMEM),
         ),
         scratch_shapes=[
@@ -367,71 +367,26 @@
             dma((4,)), dma((4,)), dma((2,)), dma((2,)), dma((NG,)), dma((NG,)),
             dma((2 * NV + 1,)), dma((2 * NV + 1,)), dma((3,)), dma((3,)),
         ],
-        compiler_params=pltpu.CompilerParams(collective_id=0, has_side_effects=True),
+        compiler_params=pltpu.CompilerParams(
+            collective_id=0, has_side_effects=True, vmem_limit_bytes=51 << 20
+        ),
         name="exchange",
     )(widths, hydro, face)
 
 
-def update(hydro, face, halo, radial, polar, diffusion, conserved, faces_out, s, band):
-    f = pl.program_id(0)
+def update(
+    hydro, face, halo, radial, polar, diffusion, conserved, faces_out,
+    s, co, fo, store_sem,
+):
     row = lax.axis_index("row")
-    shift = (120 - 16 * f) % 128
     lane = lanes((8, 128))
     sub = sublanes((8, 128))
     left, right = lane < 8, lane >= 120
-
-    def merged(raw0, raw1, packed):
-        p = pltpu.roll(packed, shift, 1)
-        return jnp.where(left, p, raw0), jnp.where(right, p, raw1)
-
-    def put(r, at, raw, packed):
-        a, b = merged(raw[:, 0:128], raw[:, 128:256], packed)
-        s[r, at:at + 8, 0:128] = a
-        s[r, at:at + 8, 128:256] = b
-
-    def edge_row(i):
-        r = ROWS + 2 + (i - 2) if i >= 2 else i
-        for j in (0, 8):
-            put(r, j, radial[0, i, j:j + 8, :], polar[ROWS + i, j:j + 8, :])
-
-    def clear_row(i):
-        r = ROWS + 2 + (i - 2) if i >= 2 else i
-        s[r] = jnp.zeros((CELLS + 8, THETA), F32)
-
-    @pl.when(f == 0)
-    def _():
-        i0 = lax.broadcasted_iota(jnp.int32, (THETA, THETA), 0)
-        i1 = lax.broadcasted_iota(jnp.int32, (THETA, THETA), 1)
-        apart = jnp.abs(i0 - i1)
-        band[...] = jnp.where(apart == 1, 16.0, jnp.where(apart == 2, -1.0, 0.0)).astype(jnp.bfloat16)
-
-    @pl.when(row > 0)
-    def _():
-        edge_row(0)
-        edge_row(1)
-
-    @pl.when(row == 0)
-    def _():
-        clear_row(0)
-        clear_row(1)
-
-    @pl.when(row < NROW - 1)
-    def _():
-        edge_row(2)
-        edge_row(3)
-
-    @pl.when(row == NROW - 1)
-    def _():
-        clear_row(2)
-        clear_row(3)
-
-    def fill(ref):
-        def step(r, carry):
-            for j in (0, 8):
-                put(r + 2, j, ref[0, r, j:j + 8, :], polar[r, j:j + 8, :])
-            put(r + 2, 16, halo[0, r], polar[r, 16:24, :])
-            return carry
-        lax.fori_loop(0, ROWS, step, 0, unroll=4)
+    i0 = lax.broadcasted_iota(jnp.int32, (THETA, THETA), 0)
+    i1 = lax.broadcasted_iota(jnp.int32, (THETA, THETA), 1)
+    apart = jnp.abs(i0 - i1)
+    band = jnp.where(apart == 0, -90.0, jnp.where(apart == 1, 16.0, jnp.where(apart == 2, -1.0, 0.0)))
+    band = band.astype(jnp.bfloat16)
 
     def around(t0, t1, h, k):
         if k > 0:
@@ -442,19 +397,51 @@
         a, b, c = (pltpu.roll(t, -k, 0) for t in (t0, t1, h))
         return jnp.where(edge, c, a), jnp.where(edge, a, b)
 
-    @pl.when(f < NV)
-    def _():
-        fill(hydro)
-        diff = diffusion[pl.ds(f, 1), :] * (1.0 / 12.0)
-        batch = 4
+    def fill(f, ref, k):
+        shift = (120 - 16 * f) % 128
+
+        def put(r, at, raw, packed):
+            p = pltpu.roll(packed, shift, 1)
+            s[r, at:at + 8, 0:128] = jnp.where(left, p, raw[:, 0:128])
+            s[r, at:at + 8, 128:256] = jnp.where(right, p, raw[:, 128:256])
+
+        def edge_row(i):
+            r = ROWS + i if i >= 2 else i
+            for j in (0, 8):
+                put(r, j, radial[min(f, NV), i, j:j + 8, :], polar[ROWS + i, j:j + 8, :])
+
+        if f <= NV:
+            for side, wide in ((row > 0, (0, 1)), (row < NROW - 1, (2, 3))):
+                @pl.when(side)
+                def _():
+                    for i in wide:
+                        edge_row(i)
+
+                @pl.when(jnp.logical_not(side))
+                def _():
+                    for i in wide:
+                        s[ROWS + i if i >= 2 else i] = jnp.zeros((CELLS + 8, THETA), F32)
+
+        def step(r, carry):
+            for j in (0, 8):
+                put(r + 2, j, ref[k, r, j:j + 8, :], polar[r, j:j + 8, :])
+            if f < NV or f == NV + 2:
+                put(r + 2, 16, halo[min(f, NV), r], polar[r, 16:24, :])
+            return carry
+        lax.fori_loop(0, ROWS, step, 0, unroll=8)
+
+    for f in range(NV):
+        fill(f, hydro, f)
+        diff = diffusion[f:f + 1, :] * (1.0 / 12.0)
+        batch = 8
 
         def step(block, carry):
             r0 = block * batch
             centre = jnp.concatenate([s[r0 + i + 2, 0:CELLS, :] for i in range(batch)], 0)
             high = centre.astype(jnp.bfloat16)
             rest = (centre - high.astype(F32)).astype(jnp.bfloat16)
-            theta = jnp.dot(high, band[...], preferred_element_type=F32)
-            theta = theta + jnp.dot(rest, band[...], preferred_element_type=F32)
+            theta = jnp.dot(high, band, preferred_element_type=F32)
+            theta = theta + jnp.dot(rest, band, preferred_element_type=F32)
             for i in range(batch):
                 r = r0 + i + 2
                 for half in range(2):
@@ -466,86 +453,62 @@
                         at = slice(8 * j, 8 * j + 8)
                         near = (n1[j] + p1[j]) + (s[r - 1, at, ln] + s[r + 1, at, ln])
                         far = (n2[j] + p2[j]) + (s[r - 2, at, ln] + s[r + 2, at, ln])
-                        change = 16.0 * near - far - 90.0 * t[j]
+                        change = 16.0 * near - far
                         change = change + theta[16 * i + 8 * j:16 * i + 8 * j + 8, ln]
-                        conserved[0, r0 + i, at, ln] = t[j] + diff[:, ln] * change
+                        co[f, r0 + i, at, ln] = t[j] + diff[:, ln] * change
             return carry
 
         lax.fori_loop(0, ROWS // batch, step, 0)
-
-    @pl.when(f >= NV)
-    def _():
-        fill(face)
-
-        def copy(r, carry):
-            faces_out[0, r] = s[r + 2, 0:CELLS, :]
+        pltpu.make_async_copy(co.at[f], conserved.at[f], store_sem.at[f]).start()
+
+    for k in range(NF):
+        f = NV + k
+        fill(f, face, k)
+
+        def step(r, carry):
+            fo[k, r] = s[r + 2, 0:CELLS, :]
+            if k == 0:
+                co[f, r] = 0.5 * (s[r + 2, 0:CELLS, :] + s[r + 3, 0:CELLS, :])
+            elif k == 1:
+                for j in (0, 8):
+                    a, b = s[r + 2, j:j + 8, 0:128], s[r + 2, j:j + 8, 128:256]
+                    ra, rb = pltpu.roll(a, 127, 1), pltpu.roll(b, 127, 1)
+                    co[f, r, j:j + 8, 0:128] = 0.5 * (a + jnp.where(lane == 127, rb, ra))
+                    co[f, r, j:j + 8, 128:256] = 0.5 * (b + jnp.where(lane == 127, 0.0, rb))
+            else:
+                for half in range(2):
+                    ln = slice(128 * half, 128 * half + 128)
+                    t = [s[r + 2, 8 * j:8 * j + 8, ln] for j in range(3)]
+                    n1 = around(*t, 1)
+                    for j in range(2):
+                        co[f, r, 8 * j:8 * j + 8, ln] = 0.5 * (t[j] + n1[j])
             return carry
-        lax.fori_loop(0, ROWS, copy, 0, unroll=4)
-
-    @pl.when(f == NV)
-    def _():
-        def step(r, carry):
-            conserved[0, r] = 0.5 * (s[r + 2, 0:CELLS, :] + s[r + 3, 0:CELLS, :])
-            return carry
-        lax.fori_loop(0, ROWS, step, 0, unroll=4)
-
-    @pl.when(f == NV + 1)
-    def _():
-        def step(r, carry):
-            for j in (0, 8):
-                a, b = s[r + 2, j:j + 8, 0:128], s[r + 2, j:j + 8, 128:256]
-                ra, rb = pltpu.roll(a, 127, 1), pltpu.roll(b, 127, 1)
-                conserved[0, r, j:j + 8, 0:128] = 0.5 * (a + jnp.where(lane == 127, rb, ra))
-                conserved[0, r, j:j + 8, 128:256] = 0.5 * (b + jnp.where(lane == 127, 0.0, rb))
-            return carry
-        lax.fori_loop(0, ROWS, step, 0, unroll=4)
-
-    @pl.when(f == NV + 2)
-    def _():
-        def step(r, carry):
-            for half in range(2):
-                ln = slice(128 * half, 128 * half + 128)
-                t = [s[r + 2, 8 * j:8 * j + 8, ln] for j in range(3)]
-                n1 = around(*t, 1)
-                for j in range(2):
-                    conserved[0, r, 8 * j:8 * j + 8, ln] = 0.5 * (t[j] + n1[j])
-            return carry
-        lax.fori_loop(0, ROWS, step, 0, unroll=4)
+        lax.fori_loop(0, ROWS, step, 0, unroll=8)
+        pltpu.make_async_copy(co.at[f], conserved.at[f], store_sem.at[f]).start()
+        pltpu.make_async_copy(fo.at[k], faces_out.at[k], store_sem.at[FIELDS + k]).start()
+
+    for f in range(FIELDS):
+        pltpu.make_async_copy(co.at[f], conserved.at[f], store_sem.at[f]).wait()
+    for k in range(NF):
+        pltpu.make_async_copy(fo.at[k], faces_out.at[k], store_sem.at[FIELDS + k]).wait()
 
 
 def run_update(hydro, face, halo, radial, polar, diffusion):
-    def hyd(f):
-        return (jnp.minimum(f, NV - 1), 0, 0, 0)
-
-    def fac(f):
-        return (jnp.maximum(f - NV, 0), 0, 0, 0)
-
-    def six(f):
-        return (jnp.where(f == NV + 2, NV, jnp.minimum(f, NV)), 0, 0, 0)
-
     return pl.pallas_call(
         update,
-        grid=(FIELDS,),
         out_shape=(
             jax.ShapeDtypeStruct((FIELDS, ROWS, CELLS, THETA), F32),
             jax.ShapeDtypeStruct((NF, ROWS, CELLS, THETA), F32),
         ),
-        in_specs=[
-            pl.BlockSpec((1, ROWS, CELLS, THETA), hyd),
-            pl.BlockSpec((1, ROWS, CELLS, THETA), fac),
-            pl.BlockSpec((1, ROWS, 8, THETA), six),
-            pl.BlockSpec((1, 4, CELLS, THETA), six),
-            pl.BlockSpec((ROWS + 4, CELLS + 8, 128), lambda f: (0, 0, 0)),
-            pl.BlockSpec((NV, THETA), lambda f: (0, 0)),
-        ],
-        out_specs=(
-            pl.BlockSpec((1, ROWS, CELLS, THETA), lambda f: (f, 0, 0, 0)),
-            pl.BlockSpec((1, ROWS, CELLS, THETA), fac),
-        ),
+        in_specs=[pl.BlockSpec(memory_space=pltpu.VMEM)] * 6,
+        out_specs=(pl.BlockSpec(memory_space=pltpu.HBM), pl.BlockSpec(memory_space=pltpu.HBM)),
         scratch_shapes=[
             pltpu.VMEM((ROWS + 4, CELLS + 8, THETA), F32),
-            pltpu.VMEM((THETA, THETA), jnp.bfloat16),
+            pltpu.VMEM((FIELDS, ROWS, CELLS, THETA), F32),
+            pltpu.VMEM((NF, ROWS, CELLS, THETA), F32),
+            pltpu.SemaphoreType.DMA((FIELDS + NF,)),
         ],
+        compiler_params=pltpu.CompilerParams(vmem_limit_bytes=24 << 20),
         name="update",
     )(hydro, face, halo, radial, polar, diffusion)
 

time: 49.7 us -> 41.9 us (0.84)
  Pallas kernels: 48.9 us -> 39.6 us
  local copies, waits for them, and re-layouts: 0 us -> 1.5 us
    pallas_call x1, Pallas kernels: 17.7 us -> 9.45 us  [run_update(): pl.pallas_call(update, out_shape=(jax.ShapeDtypeStruct((FIELDS, ROWS, CEL...]
    unnamed x0 -> x8, local copies, waits for them, and re-layouts: none -> 1.5 us
    pallas_call x1, Pallas kernels: 31.1 us -> 30.1 us  [run_exchange(): pl.pallas_call(exchange, out_shape=(jax.ShapeDtypeStruct((NV + 1, ROWS, 8...]
where the time goes in v2:
time: 41.9 us; the launch traced here: 41.7 us
  Pallas kernels  39.6 us (95%)
  local copies, waits for them, and re-layouts  1.5 us (4%)
  between operations  0.69 us (2%)
    pallas_call x1, Pallas kernels, run_exchange(): pl.pallas_call(exchange, out_shape=(jax.ShapeDtypeStruct((NV + 1, ROWS, 8...  30.1 us
    pallas_call x1, Pallas kernels, run_update(): pl.pallas_call(update, out_shape=(jax.ShapeDtypeStruct((FIELDS, ROWS, CEL...  9.45 us
    unnamed x8, local copies, waits for them, and re-layouts  1.5 us

profile of v2, /device:TPU:1, one launch (start us, length us, event | category | flops | bytes accessed | tf_op | source)
XLA Modules:
  0.0 41.7 jit_solution(10623996486692552235)
XLA Ops:
  0.6 0.0 copy-start.1
  0.6 0.0 copy-start
  0.6 0.0 copy-start.3
  0.7 0.8 %copy-done.3 = s32[16]{0:T(128)S(1)} copy-done((s32[16]{0:T(128)S(1)}, s32[16]{0:T(128)}, u32[]{:S(2)}) %copy-start.3) | copy-done | bytes 88
  1.5 30.1 %exchange.1 = (f32[6,32,8,256]{3,2,1,0:T(8,128)S(1)}, f32[6,4,16,256]{3,2,1,0:T(8,128)S(1)}, f32[36,24,128]{2,1,0:T(8,128)S(1)}) custom-call(s32[16]{0:T(128)S(1)} %copy-done.3, f32[5,32,16,256]{3,2,1,0:T(8,128)} %hydro.3, f32[3,32,16,256]{3,2,1,0:T(8,128)} %face.3), custom_call_target="tpu_custom_call" | custom-call | tf_op jit(solution)/shard_map/exchange/pallas_call | solution.py:336
  31.6 0.0 copy-done.1
  31.6 0.0 copy-done
  31.6 0.0 copy-start.2
  31.6 0.7 %copy-done.2 = f32[5,256]{1,0:T(8,128)S(1)} copy-done((f32[5,256]{1,0:T(8,128)S(1)}, f32[5,256]{1,0:T(8,128)}, u32[]{:S(2)}) %copy-start.2) | copy-done | bytes 5144
  32.3 9.4 %update.1 = (f32[8,32,16,256]{3,2,1,0:T(8,128)}, f32[3,32,16,256]{3,2,1,0:T(8,128)}) custom-call(f32[5,32,16,256]{3,2,1,0:T(8,128)S(1)} %copy-done, f32[3,32,16,256]{3,2,1,0:T(8,128)S(1)} %copy-done.1, f32[6,32,8,256]{3,2,1,0:T(8,128)S(1)} %get-tuple-element.5.halo, f32[6,4,16,256]{3,2,1,0:T(8,128)S(1)} %get-tuple-element.6.radial, ...), custom_call_target="tpu_custom_call" | custom-call | tf_op jit(solution)/shard_map/update/pallas_call | solution.py:497
Async XLA Ops:
  0.6 30.9 %copy-start.1 = (f32[3,32,16,256]{3,2,1,0:T(8,128)S(1)}, f32[3,32,16,256]{3,2,1,0:T(8,128)}, u32[]{:S(2)}) copy-start(f32[3,32,16,256]{3,2,1,0:T(8,128)} %face.3) | copy-start | bytes 4718596
  0.6 30.9 %copy-start = (f32[5,32,16,256]{3,2,1,0:T(8,128)S(1)}, f32[5,32,16,256]{3,2,1,0:T(8,128)}, u32[]{:S(2)}) copy-start(f32[5,32,16,256]{3,2,1,0:T(8,128)} %hydro.3) | copy-start | bytes 7864324
  0.6 0.8 %copy-start.3 = (s32[16]{0:T(128)S(1)}, s32[16]{0:T(128)}, u32[]{:S(2)}) copy-start(s32[16]{0:T(128)} %widths.1) | copy-start | bytes 196
  31.6 0.7 %copy-start.2 = (f32[5,256]{1,0:T(8,128)S(1)}, f32[5,256]{1,0:T(8,128)}, u32[]{:S(2)}) copy-start(f32[5,256]{1,0:T(8,128)} %diffusion.1) | copy-start | bytes 15364

commit v3 on v2

v3 whole, which is shorter than its diff:
```python
import jax
import jax.numpy as jnp
from jax import lax
from jax.experimental import pallas as pl
from jax.experimental.pallas import tpu as pltpu
from jax.sharding import PartitionSpec as P

F32 = jnp.float32
MESH = pl.DeviceIdType.MESH
NV, NF, FIELDS = 5, 3, 8
ROWS, CELLS, THETA = 32, 16, 256
NZ, NG, NROW = 8, 8, 4
EARLY = 5
BATCH = 8
FAR_FIRST = (4, 3, 5, 2, 6, 1, 7)


def lanes(shape):
    return lax.broadcasted_iota(jnp.int32, shape, len(shape) - 1)


def sublanes(shape):
    return lax.broadcasted_iota(jnp.int32, shape, len(shape) - 2)


def around(t0, t1, h, k, sub):
    if k > 0:
        edge = sub >= 8 - k
        a, b, c = (None if t is None else pltpu.roll(t, 8 - k, 0) for t in (t0, t1, h))
        return jnp.where(edge, b, a), jnp.where(edge, 0.0 if c is None else c, b)
    edge = sub < -k
    a, b, c = (None if t is None else pltpu.roll(t, -k, 0) for t in (t0, t1, h))
    return jnp.where(edge, 0.0 if c is None else c, a), jnp.where(edge, a, b)


def exchange(
    widths_hbm, hydro, face, diffusion_hbm, pre, even, odd, packed_out,
    hv, fv, halo, radial, la, pp, zsum, gsum, edge, first, last, first_in, last_in, la_in,
    dd, mm, widths, diffusion, small_sem,
    load_sem, q_send, q_recv, qn_send, qn_recv, qp_send, qp_recv,
    la_send, la_recv, e_send, e_recv, g_send, g_recv,
    p_send, p_recv, r_send, r_recv,
):
    row, phi = lax.axis_index("row"), lax.axis_index("phi")
    z, g = phi % NZ, phi // NZ
    nphi = NZ * NG
    after, before = (phi + 1) % nphi, (phi + nphi - 1) % nphi
    has_prev, has_next = row > 0, row < NROW - 1

    def peer(d):
        return g * NZ + (z + d) % NZ

    def group(d):
        return ((g + d) % NG) * NZ + z

    get_widths = pltpu.make_async_copy(widths_hbm, widths, small_sem.at[0])
    get_diffusion = pltpu.make_async_copy(diffusion_hbm, diffusion, small_sem.at[1])
    get_widths.start()
    loads = []
    for i in range(4):
        loads.append((
            pltpu.make_async_copy(hydro.at[:, 8 * i:8 * i + 8], hv.at[:, 8 * i + 2:8 * i + 10], load_sem.at[2 * i]),
            pltpu.make_async_copy(face.at[:, 8 * i:8 * i + 8], fv.at[:, 8 * i:8 * i + 8], load_sem.at[2 * i + 1]),
        ))
        for copy in loads[i]:
            copy.start()
    get_diffusion.start()

    zsum[:, ROWS:, :] = jnp.zeros((NZ, 8, 128), F32)
    barrier = pltpu.get_barrier_semaphore()

    def hello(r, p):
        pl.semaphore_signal(barrier, inc=1, device_id=(r, p), device_id_type=MESH)

    for d in range(1, NZ):
        hello(row, peer(d))
        hello(row, group(d))

    @pl.when(has_prev)
    def _():
        for d in range(NZ):
            hello(row - 1, peer(d))

    @pl.when(has_next)
    def _():
        for d in range(NZ):
            hello(row + 1, peer(d))

    @pl.when(z == 0)
    def _():
        hello(row, before)

    @pl.when(z == NZ - 1)
    def _():
        hello(row, after)

    for i in range(NV):
        for r in (0, 1, ROWS + 2, ROWS + 3):
            hv[i, r] = jnp.zeros((CELLS, THETA), F32)

    lane = lanes((8, 128))
    sub = sublanes((8, 128))
    low = lane < 64
    get_widths.wait()
    width = jnp.zeros((8, 128), jnp.int32)
    for c in range(16):
        width = jnp.where(lane % 16 == c, widths[(c + 8) % 16], width)

    def pack(block, base):
        q8 = jnp.zeros((8, 128), F32)
        f8 = jnp.zeros((8, 128), F32)
        l8 = jnp.zeros((8, 128), F32)
        for i in range(8):
            r = block * 8 + i
            sums, local = [], []
            for j in range(2):
                p = None
                for f in range(FIELDS):
                    ref, k, at = (hv, f, r + 2) if f < NV else (fv, f - NV, r)
                    t0 = ref[k, at, 8 * j:8 * j + 8, 0:128]
                    t1 = ref[k, at, 8 * j:8 * j + 8, 128:256]
                    t = jnp.where(low, t0, t1)
                    shift = (8 + 16 * f) % 128
                    t = pltpu.roll(t, shift, 1)
                    p = t if p is None else jnp.where(lane // 16 == f, t, p)
                pp[r, 8 * j:8 * j + 8, :] = p
                s2 = p + jnp.where(sub % 2 == 0, pltpu.roll(p, 7, 0), pltpu.roll(p, 1, 0))
                s4 = s2 + jnp.where(sub % 4 < 2, pltpu.roll(s2, 6, 0), pltpu.roll(s2, 2, 0))
                s8 = s4 + pltpu.roll(s4, 4, 0)
                sums.append(s8)
                local.append((s2, s4, s8))
            s16 = sums[0] + sums[1]
            for j, (s2, s4, s8) in enumerate(local):
                mean = jnp.where(width == 2, s2 * 0.5, s16 * 0.0625)
                mean = jnp.where(width == 4, s4 * 0.25, mean)
                mean = jnp.where(width == 8, s8 * 0.125, mean)
                la[r, 8 * j:8 * j + 8, :] = mean
                local[j] = mean
            q8 = jnp.where(sub == i, s16, q8)
            f8 = jnp.where(sub == i, pltpu.roll(local[0], i, 0) if i else local[0], f8)
            l8 = jnp.where(sub == i, pltpu.roll(local[1], (i + 1) % 8, 0) if i < 7 else local[1], l8)
        at = pl.ds(pl.multiple_of(block * 8, 8), 8)
        zsum[z, at, :] = q8
        first[at, :] = f8
        last[at, :] = l8
        return base

    for i in range(4):
        for copy in loads[i]:
            copy.wait()
        pack(i, 0)

    hellos = 2 * (NZ - 1) + NZ * (has_prev.astype(jnp.int32) + has_next.astype(jnp.int32))
    hellos += (z == 0).astype(jnp.int32) + (z == NZ - 1).astype(jnp.int32)
    pl.semaphore_wait(barrier, hellos)

    def remote(src, dst, ssem, rsem, r, p):
        return pltpu.make_async_remote_copy(
            src_ref=src, dst_ref=dst, send_sem=ssem, recv_sem=rsem,
            device_id=(r, p), device_id_type=MESH,
        )

    def q_copy(d):
        ref = zsum.at[z, 0:ROWS, :]
        return remote(ref, ref, q_send.at[d], q_recv.at[d], row, peer(d))

    def q_down(d):
        return remote(
            zsum.at[z, 0:2, :], zsum.at[z, ROWS + 2:ROWS + 4, :],
            qn_send.at[d], qn_recv.at[d], row - 1, peer(d),
        )

    def q_up(d):
        return remote(
            zsum.at[z, ROWS - 2:ROWS, :], zsum.at[z, ROWS:ROWS + 2, :],
            qp_send.at[d], qp_recv.at[d], row + 1, peer(d),
        )

    for d in FAR_FIRST:
        q_copy(d).start()

    @pl.when(has_prev)
    def _():
        for d in FAR_FIRST + (0,):
            q_down(d).start()

    @pl.when(has_next)
    def _():
        for d in FAR_FIRST + (0,):
            q_up(d).start()

    edge_first = remote(first, first_in, la_send.at[0], la_recv.at[0], row, before)
    edge_last = remote(last, last_in, la_send.at[1], la_recv.at[1], row, after)
    edge_first.start()
    edge_last.start()
    la_down = remote(la.at[0:2], la_in.at[2:4], la_send.at[2], la_recv.at[2], row - 1, phi)
    la_up = remote(la.at[ROWS - 2:ROWS], la_in.at[0:2], la_send.at[3], la_recv.at[3], row + 1, phi)

    down = [remote(hv.at[:, 2:4], radial.at[0:NV, 2:4], r_send.at[0], r_recv.at[0], row - 1, phi)]
    down += [remote(fv.at[0, 0:1], radial.at[NV, 2:3], r_send.at[1], r_recv.at[1], row - 1, phi)]
    up = [remote(hv.at[:, ROWS:ROWS + 2], radial.at[0:NV, 0:2], r_send.at[2], r_recv.at[2], row + 1, phi)]

    @pl.when(has_prev)
    def _():
        la_down.start()
        for copy in down:
            copy.start()

    @pl.when(has_next)
    def _():
        la_up.start()
        for copy in up:
            copy.start()

    bulk = []
    for i in range(NV):
        bulk.append(remote(
            hv.at[i, 2:ROWS + 2, CELLS - 2:CELLS, :], halo.at[i, :, 6:8, :],
            p_send.at[2 * i], p_recv.at[2 * i], row, after,
        ))
        bulk.append(remote(
            hv.at[i, 2:ROWS + 2, 0:2, :], halo.at[i, :, 0:2, :],
            p_send.at[2 * i + 1], p_recv.at[2 * i + 1], row, before,
        ))
    bulk.append(remote(
        fv.at[2, :, 0:1, :], halo.at[NV, :, 0:1, :],
        p_send.at[2 * NV], p_recv.at[2 * NV], row, before,
    ))
    for copy in bulk[:2 * EARLY]:
        copy.start()

    get_diffusion.wait()
    i0 = lax.broadcasted_iota(jnp.int32, (THETA, THETA), 0)
    i1 = lax.broadcasted_iota(jnp.int32, (THETA, THETA), 1)
    apart = jnp.abs(i0 - i1)
    band = jnp.where(apart == 0, -90.0, jnp.where(apart == 1, 16.0, jnp.where(apart == 2, -1.0, 0.0)))
    band = band.astype(jnp.bfloat16)

    def raw_field(f):
        diff = diffusion[f:f + 1, :] * (1.0 / 12.0)

        def step(block, carry):
            r0 = block * BATCH
            centre = jnp.concatenate([hv[f, r0 + i + 2] for i in range(BATCH)], 0)
            high = centre.astype(jnp.bfloat16)
            rest = (centre - high.astype(F32)).astype(jnp.bfloat16)
            theta = jnp.dot(high, band, preferred_element_type=F32)
            theta = theta + jnp.dot(rest, band, preferred_element_type=F32)
            for i in range(BATCH):
                r = r0 + i + 2
                for half in range(2):
                    ln = slice(128 * half, 128 * half + 128)
                    t = [hv[f, r, 8 * j:8 * j + 8, ln] for j in range(2)] + [None]
                    n1, n2 = around(*t, 1, sub), around(*t, 2, sub)
                    p1, p2 = around(*t, -1, sub), around(*t, -2, sub)
                    for j in range(2):
                        at = slice(8 * j, 8 * j + 8)
                        near = (n1[j] + p1[j]) + (hv[f, r - 1, at, ln] + hv[f, r + 1, at, ln])
                        far = (n2[j] + p2[j]) + (hv[f, r - 2, at, ln] + hv[f, r + 2, at, ln])
                        change = 16.0 * near - far
                        change = change + theta[16 * i + 8 * j:16 * i + 8 * j + 8, ln]
                        pre[f, r0 + i, at, ln] = t[j] + diff[:, ln] * change
            return carry

        lax.fori_loop(0, ROWS // BATCH, step, 0)

    def raw_faces():
        def step(r, carry):
            for j in (0, 8):
                a, b = fv[1, r, j:j + 8, 0:128], fv[1, r, j:j + 8, 128:256]
                ra, rb = pltpu.roll(a, 127, 1), pltpu.roll(b, 127, 1)
                pre[NV + 1, r, j:j + 8, 0:128] = 0.5 * (a + jnp.where(lane == 127, rb, ra))
                pre[NV + 1, r, j:j + 8, 128:256] = 0.5 * (b + jnp.where(lane == 127, 0.0, rb))
            for half in range(2):
                ln = slice(128 * half, 128 * half + 128)
                t = [fv[2, r, 8 * j:8 * j + 8, ln] for j in range(2)]
                n1 = around(t[0], t[1], None, 1, sub)
                for j in range(2):
                    pre[NV + 2, r, 8 * j:8 * j + 8, ln] = 0.5 * (t[j] + n1[j])
            return carry
        lax.fori_loop(0, ROWS, step, 0, unroll=4)

        def mean_step(r, carry):
            pre[NV, r] = 0.5 * (fv[0, r] + fv[0, r + 1])
            return carry
        lax.fori_loop(0, ROWS - 1, mean_step, 0)
        pre[NV, ROWS - 1] = 0.5 * fv[0, ROWS - 1]

    for f in range(NV):
        raw_field(f)

    for d in FAR_FIRST:
        q_copy(d).wait_recv()

    @pl.when(has_prev)
    def _():
        for d in FAR_FIRST + (0,):
            q_up(d).wait_recv()

    @pl.when(has_next)
    def _():
        for d in FAR_FIRST + (0,):
            q_down(d).wait_recv()

    def z_sums(at):
        pair, quad = (at // 2) * 2, (at // 4) * 4
        s32 = zsum[pair] + zsum[pair + 1]
        s64 = (zsum[quad] + zsum[quad + 1]) + (zsum[quad + 2] + zsum[quad + 3])
        return s32, s64

    tall = (ROWS + 8, 128)
    wide = jnp.broadcast_to(width[0:1], tall)
    total = zsum[0]
    for i in range(1, NZ):
        total = total + zsum[i]
    gsum[g] = total

    def g_copy(d):
        return remote(gsum.at[g], gsum.at[g], g_send.at[d], g_recv.at[d], row, group(d))

    for d in (5, 3, 7, 1, 6, 2, 4):
        g_copy(d).start()

    s32p, s64p = z_sums((z + NZ - 1) % NZ)
    s32n, s64n = z_sums((z + 1) % NZ)
    edge[0] = jnp.where(wide == 32, s32p * (1 / 32), s64p * (1 / 64))[:ROWS]
    edge[1] = jnp.where(wide == 32, s32n * (1 / 32), s64n * (1 / 64))[:ROWS]
    edge_up = remote(edge.at[0], edge.at[2], e_send.at[0], e_recv.at[0], row, group(1))
    edge_down = remote(edge.at[1], edge.at[3], e_send.at[1], e_recv.at[1], row, group(NG - 1))
    edge_up.start()
    edge_down.start()

    for copy in bulk[2 * EARLY:]:
        copy.start()

    raw_faces()

    seg, m = lane // 16, lane % 16
    is_even = seg % 2 == 0
    diff_even = jnp.zeros((8, 128), F32)
    diff_odd = jnp.zeros((8, 128), F32)
    for f in range(NV):
        t = jnp.where(low, diffusion[f:f + 1, 0:128], diffusion[f:f + 1, 128:256])
        t = pltpu.roll(jnp.broadcast_to(t, (8, 128)), (8 + 16 * f) % 128, 1) * (1.0 / 12.0)
        near_f = (lane - 16 * f + 2 + 128) % 128 < 20
        if f % 2 == 0:
            diff_even = jnp.where(near_f, t, diff_even)
        else:
            diff_odd = jnp.where(near_f, t, diff_odd)
    own = jnp.where(is_even, diff_even, diff_odd)
    out = jnp.where(is_even, diff_odd, diff_even)
    fluid = seg < NV
    zero = jnp.zeros((8, 128), F32)
    c0 = jnp.where(fluid, 1.0 - 90.0 * own, 0.5)
    c1 = jnp.where(fluid, 16.0 * own, zero)
    c2 = jnp.where(fluid, -own, zero)
    c_row = jnp.where(seg == NV, 0.5, zero)
    c_cell = jnp.where(seg == NV + 2, 0.5, zero)
    k1p = jnp.where(m % 8 == 0, zero, c1)
    k1n = jnp.where(m % 8 == 7, zero, c1 + jnp.where(seg == NV + 1, 0.5, zero))
    k2p = jnp.where(m % 8 < 2, zero, c2)
    k2n = jnp.where(m % 8 > 5, zero, c2)
    from_left = (seg + 7) % 8
    from_right = (seg + 1) % 8
    left_fluid, right_fluid = from_left < NV, from_right < NV
    s1p = jnp.where(jnp.logical_and(m == 0, left_fluid), 16.0 * out, zero)
    s2p = jnp.where(jnp.logical_and(m < 2, left_fluid), -out, zero)
    s1n = jnp.where(jnp.logical_and(m == 15, right_fluid), 16.0 * out, zero)
    s1n = jnp.where(jnp.logical_and(m == 15, from_right == NV + 1), 0.5, s1n)
    s2n = jnp.where(jnp.logical_and(m > 13, right_fluid), -out, zero)

    inner = (lane >= 8, lane < 120)

    @pl.when(has_prev)
    def _():
        for copy in up:
            copy.wait_recv()
        for f in range(NV):
            for half in range(2):
                ln = slice(128 * half, 128 * half + 128)
                diff = diffusion[f:f + 1, ln] * (1.0 / 12.0)
                for at in (slice(0, 8), slice(8, 16)):
                    b2, b1 = (jnp.where(inner[half], radial[f, i, at, ln], 0.0) for i in (0, 1))
                    pre[f, 0, at, ln] = pre[f, 0, at, ln] + diff * (16.0 * b1 - b2)
                    pre[f, 1, at, ln] = pre[f, 1, at, ln] - diff * b1

    @pl.when(has_next)
    def _():
        for copy in down:
            copy.wait_recv()
        for half in range(2):
            ln = slice(128 * half, 128 * half + 128)
            for at in (slice(0, 8), slice(8, 16)):
                for f in range(NV):
                    diff = diffusion[f:f + 1, ln] * (1.0 / 12.0)
                    b1, b2 = (jnp.where(inner[half], radial[f, i, at, ln], 0.0) for i in (2, 3))
                    e, e1 = ROWS - 1, ROWS - 2
                    pre[f, e, at, ln] = pre[f, e, at, ln] + diff * (16.0 * b1 - b2)
                    pre[f, e1, at, ln] = pre[f, e1, at, ln] - diff * b1
                b = jnp.where(inner[half], radial[NV, 2, at, ln], 0.0)
                pre[NV, ROWS - 1, at, ln] = pre[NV, ROWS - 1, at, ln] + 0.5 * b

    a1 = jnp.where(sub == 0, 16.0, zero)
    a2 = jnp.where(sub < 2, -1.0, zero)
    b1 = jnp.where(sub == 7, 16.0, zero)
    b2 = jnp.where(sub > 5, -1.0, zero)
    for f in range(NV):
        bulk[2 * f].wait_recv()
        bulk[2 * f + 1].wait_recv()
        diffs = [diffusion[f:f + 1, 128 * half:128 * half + 128] * (1.0 / 12.0) for half in range(2)]

        def step(r, carry):
            for half in range(2):
                ln = slice(128 * half, 128 * half + 128)
                h = jnp.where(inner[half], halo[f, r, :, ln], 0.0) * diffs[half]
                head = a1 * pltpu.roll(h, 1, 0) + a2 * pltpu.roll(h, 2, 0)
                tail = b1 * pltpu.roll(h, 7, 0) + b2 * pltpu.roll(h, 6, 0)
                pre[f, r, 0:8, ln] = pre[f, r, 0:8, ln] + head
                pre[f, r, 8:16, ln] = pre[f, r, 8:16, ln] + tail
            return carry
        lax.fori_loop(0, ROWS, step, 0, unroll=8)
    bulk[2 * NV].wait_recv()

    def face_step(r, carry):
        for half in range(2):
            ln = slice(128 * half, 128 * half + 128)
            h = pltpu.roll(halo[NV, r, :, ln], 7, 0)
            h = jnp.where(jnp.logical_and(inner[half], sub == 7), 0.5 * h, 0.0)
            pre[NV + 2, r, 8:16, ln] = pre[NV + 2, r, 8:16, ln] + h
        return carry
    lax.fori_loop(0, ROWS, face_step, 0, unroll=8)

    for d in (5, 3, 7, 1, 6, 2, 4):
        g_copy(d).wait_recv()
    edge_up.wait_recv()
    edge_down.wait_recv()
    edge_first.wait_recv()
    edge_last.wait_recv()

    whole = gsum[0]
    for i in range(1, NG):
        whole = whole + gsum[i]
    whole = whole * (1 / 1024)

    def g_means(at, small):
        pair, quad = (at // 2) * 2, (at // 4) * 4
        mean = jnp.where(wide == 128, gsum[at] * (1 / 128), small)
        mean = jnp.where(wide == 256, (gsum[pair] + gsum[pair + 1]) * (1 / 256), mean)
        four = (gsum[quad] + gsum[quad + 1]) + (gsum[quad + 2] + gsum[quad + 3])
        mean = jnp.where(wide == 512, four * (1 / 512), mean)
        return jnp.where(wide == 1024, whole, mean)

    s32, s64 = z_sums(z)
    mm[0] = g_means(g, jnp.where(wide == 32, s32 * (1 / 32), s64 * (1 / 64)))
    gp = jnp.where(z == 0, (g + NG - 1) % NG, g)
    gn = jnp.where(z == NZ - 1, (g + 1) % NG, g)
    pad = jnp.zeros((8, 128), F32)
    ep = jnp.concatenate([jnp.where(z == 0, edge[2], edge[0]), pad])
    en = jnp.concatenate([jnp.where(z == NZ - 1, edge[3], edge[1]), pad])
    mm[1] = jnp.where(wide <= 16, jnp.concatenate([last_in[...], pad]), g_means(gp, ep))
    mm[2] = jnp.where(wide <= 16, jnp.concatenate([first_in[...], pad]), g_means(gn, en))
    narrow = width <= 16

    def differ(r, carry):
        mean = jnp.broadcast_to(mm[0, pl.ds(r, 1), :], (8, 128))
        for j in (0, 8):
            a = jnp.where(narrow, la[r, j:j + 8, :], mean)
            packed_out[r, j:j + 8, :] = a
            dd[r + 2, j:j + 8, :] = a - pp[r, j:j + 8, :]
        prev = jnp.broadcast_to(mm[1, pl.ds(r, 1), :], (8, 128))
        follow = jnp.broadcast_to(mm[2, pl.ds(r, 1), :], (8, 128))
        dd[r + 2, 16:24, :] = jnp.where(sub < 4, follow, prev)
        return carry

    lax.fori_loop(0, ROWS, differ, 0, unroll=8)

    for side, wait, which in ((has_prev, la_up, (0, 1)), (has_next, la_down, (2, 3))):
        @pl.when(side)
        def _():
            wait.wait_recv()
            for i in which:
                mean = jnp.broadcast_to(mm[0, ROWS + i:ROWS + i + 1, :], (8, 128))
                for j in (0, 8):
                    a = jnp.where(narrow, la_in[i, j:j + 8, :], mean)
                    dd[i if i < 2 else ROWS + i, j:j + 8, :] = a

        @pl.when(jnp.logical_not(side))
        def _():
            for i in which:
                dd[i if i < 2 else ROWS + i, 0:16, :] = jnp.zeros((16, 128), F32)

    def correct(r, carry):
        t = [dd[r + 2, 8 * j:8 * j + 8, :] for j in range(3)]
        n1, n2 = around(*t, 1, sub), around(*t, 2, sub)
        p1, p2 = around(*t, -1, sub), around(*t, -2, sub)
        for j in range(2):
            at = slice(8 * j, 8 * j + 8)
            d = t[j]
            below = dd[r + 3, at, :]
            near = (n1[j] + p1[j]) + (dd[r + 1, at, :] + below)
            far = (n2[j] + p2[j]) + (dd[r, at, :] + dd[r + 4, at, :])
            lp1, lp2 = pltpu.roll(d, 1, 1), pltpu.roll(d, 2, 1)
            ln1, ln2 = pltpu.roll(d, 127, 1), pltpu.roll(d, 126, 1)
            base = (c0 * d + c1 * near) + (c2 * far + c_row * below)
            base = base + (c_cell * n1[j] + k1p * lp1) + (k1n * ln1 + k2p * lp2) + k2n * ln2
            side = (s1p * lp1 + s2p * lp2) + (s1n * ln1 + s2n * ln2)
            even[r, at, :] = jnp.where(is_even, base, side)
            odd[r, at, :] = jnp.where(is_even, side, base)
        return carry

    lax.fori_loop(0, ROWS, correct, 0, unroll=4)

    for d in FAR_FIRST:
        q_copy(d).wait_send()
        g_copy(d).wait_send()
    for copy in bulk + [edge_up, edge_down, edge_first, edge_last]:
        copy.wait_send()

    @pl.when(has_prev)
    def _():
        la_down.wait_send()
        for copy in down:
            copy.wait_send()
        for d in range(NZ):
            q_down(d).wait_send()

    @pl.when(has_next)
    def _():
        la_up.wait_send()
        for copy in up:
            copy.wait_send()
        for d in range(NZ):
            q_up(d).wait_send()


def run_exchange(widths, hydro, face, diffusion):
    dma = pltpu.SemaphoreType.DMA
    packed = jax.ShapeDtypeStruct((ROWS, CELLS, 128), F32)
    return pl.pallas_call(
        exchange,
        out_shape=(jax.ShapeDtypeStruct((FIELDS, ROWS, CELLS, THETA), F32), packed, packed, packed),
        in_specs=[pl.BlockSpec(memory_space=pltpu.HBM)] * 4,
        out_specs=(pl.BlockSpec(memory_space=pltpu.VMEM),) * 4,
        scratch_shapes=[
            pltpu.VMEM((NV, ROWS + 4, CELLS, THETA), F32),
            pltpu.VMEM((NF, ROWS, CELLS, THETA), F32),
            pltpu.VMEM((NV + 1, ROWS, 8, THETA), F32),
            pltpu.VMEM((NV + 1, 4, CELLS, THETA), F32),
            pltpu.VMEM((ROWS, CELLS, 128), F32),
            pltpu.VMEM((ROWS, CELLS, 128), F32),
            pltpu.VMEM((NZ, ROWS + 8, 128), F32),
            pltpu.VMEM((NG, ROWS + 8, 128), F32),
            pltpu.VMEM((4, ROWS, 128), F32),
            pltpu.VMEM((ROWS, 128), F32),
            pltpu.VMEM((ROWS, 128), F32),
            pltpu.VMEM((ROWS, 128), F32),
            pltpu.VMEM((ROWS, 128), F32),
            pltpu.VMEM((4, CELLS, 128), F32),
            pltpu.VMEM((ROWS + 4, CELLS + 8, 128), F32),
            pltpu.VMEM((3, ROWS + 8, 128), F32),
            pltpu.SMEM((16,), jnp.int32),
            pltpu.VMEM((NV, THETA), F32),
            dma((2,)),
            dma((8,)),
            dma((NZ,)), dma((NZ,)), dma((NZ,)), dma((NZ,)), dma((NZ,)), dma((NZ,)),
            dma((4,)), dma((4,)), dma((2,)), dma((2,)), dma((NG,)), dma((NG,)),
            dma((2 * NV + 1,)), dma((2 * NV + 1,)), dma((3,)), dma((3,)),
        ],
        compiler_params=pltpu.CompilerParams(
            collective_id=0, has_side_effects=True, vmem_limit_bytes=20 << 20
        ),
        name="exchange",
    )(*(pltpu.with_memory_space_constraint(x, pltpu.HBM) for x in (widths, hydro, face, diffusion)))


def update(pre, even, odd, packed, face, conserved, faces_out, co, fo, store_sem):
    lane = lanes((8, 128))

    def copy(f):
        return pltpu.make_async_copy(co.at[f], conserved.at[f], store_sem.at[f])

    def face_copy(k):
        return pltpu.make_async_copy(fo.at[k], faces_out.at[k], store_sem.at[FIELDS + k])

    for f in range(FIELDS):
        shift = (120 - 16 * f) % 128
        delta = even if f % 2 == 0 else odd

        def step(r, carry):
            for j in (0, 8):
                at = slice(j, j + 8)
                p = pltpu.roll(delta[r, at, :], shift, 1)
                co[f, r, at, 0:128] = pre[f, r, at, 0:128] + jnp.where(lane < 10, p, 0.0)
                co[f, r, at, 128:256] = pre[f, r, at, 128:256] + jnp.where(lane >= 118, p, 0.0)
                if f >= NV:
                    p = pltpu.roll(packed[r, at, :], shift, 1)
                    fo[f - NV, r, at, 0:128] = jnp.where(lane < 8, p, face[f - NV, r, at, 0:128])
                    fo[f - NV, r, at, 128:256] = jnp.where(lane >= 120, p, face[f - NV, r, at, 128:256])
            return carry

        lax.fori_loop(0, ROWS, step, 0, unroll=8)
        copy(f).start()
        if f >= NV:
            face_copy(f - NV).start()

    for f in range(FIELDS):
        copy(f).wait()
    for k in range(NF):
        face_copy(k).wait()


def run_update(pre, even, odd, packed, face):
    return pl.pallas_call(
        update,
        out_shape=(
            jax.ShapeDtypeStruct((FIELDS, ROWS, CELLS, THETA), F32),
            jax.ShapeDtypeStruct((NF, ROWS, CELLS, THETA), F32),
        ),
        in_specs=[pl.BlockSpec(memory_space=pltpu.VMEM)] * 5,
        out_specs=(pl.BlockSpec(memory_space=pltpu.HBM), pl.BlockSpec(memory_space=pltpu.HBM)),
        scratch_shapes=[
            pltpu.VMEM((FIELDS, ROWS, CELLS, THETA), F32),
            pltpu.VMEM((NF, ROWS, CELLS, THETA), F32),
            pltpu.SemaphoreType.DMA((FIELDS + NF,)),
        ],
        compiler_params=pltpu.CompilerParams(vmem_limit_bytes=16 << 20),
        name="update",
    )(pre, even, odd, packed, face)


def body(hydro, face, widths, diffusion):
    return run_update(*run_exchange(widths, hydro, face, diffusion), face)


def solution(mesh):
    spec = P(None, "row", "phi", None)
    return jax.shard_map(
        body, mesh=mesh, in_specs=(spec, spec, P(), P()), out_specs=(spec, spec), check_vma=False
    )
```

time: 41.9 us -> 35.4 us (0.84)
  Pallas kernels: 39.6 us -> 34.7 us
  local copies, waits for them, and re-layouts: 1.5 us -> 0.01 us
    pallas_call x1, Pallas kernels: 9.45 us -> 3.96 us  [run_update(): pl.pallas_call(update, out_shape=(jax.ShapeDtypeStruct((FIELDS, ROWS, CEL...]
    unnamed x8 -> x2, local copies, waits for them, and re-layouts: 1.5 us -> 0.01 us
    pallas_call x1, Pallas kernels: 30.1 us -> 30.7 us  [run_exchange(): pl.pallas_call(exchange, out_shape=(jax.ShapeDtypeStruct((FIELDS, ROWS, C...]
where the time goes in v3:
time: 35.4 us; the launch traced here: 35.3 us
  Pallas kernels  34.7 us (98%)
  between operations  0.65 us (2%)
    pallas_call x1, Pallas kernels, run_exchange(): pl.pallas_call(exchange, out_shape=(jax.ShapeDtypeStruct((FIELDS, ROWS, C...  30.7 us
    pallas_call x1, Pallas kernels, run_update(): pl.pallas_call(update, out_shape=(jax.ShapeDtypeStruct((FIELDS, ROWS, CEL...  3.96 us

profile of v3, /device:TPU:1, one launch (start us, length us, event | category | flops | bytes accessed | tf_op | source)
XLA Modules:
  0.0 35.3 jit_solution(8366474278941064056)
XLA Ops:
  0.6 0.0 copy-start
  0.6 30.7 %exchange.1 = (f32[8,32,16,256]{3,2,1,0:T(8,128)S(1)}, f32[32,16,128]{2,1,0:T(8,128)S(1)}, f32[32,16,128]{2,1,0:T(8,128)S(1)}, f32[32,16,128]{2,1,0:T(8,128)S(1)}) custom-call(s32[16]{0:T(128)} %widths_hbm.1, f32[5,32,16,256]{3,2,1,0:T(8,128)} %hydro.1, f32[3,32,16,256]{3,2,1,0:T(8,128)} %face.3, f32[5,256]{1,0:T(8,128)} %diffusion_hbm.1), custom_call_target="tpu_custom_call" | custom-call | tf_op jit(solution)/shard_map/exchange/pallas_call | solution.py:539
  31.3 0.0 copy-done
  31.4 4.0 %update.1 = (f32[8,32,16,256]{3,2,1,0:T(8,128)}, f32[3,32,16,256]{3,2,1,0:T(8,128)}) custom-call(f32[8,32,16,256]{3,2,1,0:T(8,128)S(1)} %get-tuple-element.6.pre, f32[32,16,128]{2,1,0:T(8,128)S(1)} %get-tuple-element.7.even, f32[32,16,128]{2,1,0:T(8,128)S(1)} %get-tuple-element.8.odd, f32[32,16,128]{2,1,0:T(8,128)S(1)} %get-tuple-element.9.packed, ...), custom_call_target="tpu_custom_call" | custom-call | tf_op jit(solution)/shard_map/update/pallas_call | solution.py:613
Async XLA Ops:
  0.6 30.7 %copy-start = (f32[3,32,16,256]{3,2,1,0:T(8,128)S(1)}, f32[3,32,16,256]{3,2,1,0:T(8,128)}, u32[]{:S(2)}) copy-start(f32[3,32,16,256]{3,2,1,0:T(8,128)} %face.3) | copy-start | bytes 4718596

commit v4 on v3

--- a/solution.py
+++ b/solution.py
@@ -12,6 +12,7 @@
 NZ, NG, NROW = 8, 8, 4
 EARLY = 5
 BATCH = 8
+PART = 8
 FAR_FIRST = (4, 3, 5, 2, 6, 1, 7)
 
 
@@ -327,8 +328,14 @@
     edge[1] = jnp.where(wide == 32, s32n * (1 / 32), s64n * (1 / 64))[:ROWS]
     edge_up = remote(edge.at[0], edge.at[2], e_send.at[0], e_recv.at[0], row, group(1))
     edge_down = remote(edge.at[1], edge.at[3], e_send.at[1], e_recv.at[1], row, group(NG - 1))
-    edge_up.start()
-    edge_down.start()
+
+    @pl.when(z == 0)
+    def _():
+        edge_up.start()
+
+    @pl.when(z == NZ - 1)
+    def _():
+        edge_down.start()
 
     for copy in bulk[2 * EARLY:]:
         copy.start()
@@ -432,8 +439,17 @@
 
     for d in (5, 3, 7, 1, 6, 2, 4):
         g_copy(d).wait_recv()
-    edge_up.wait_recv()
-    edge_down.wait_recv()
+
+    @pl.when(z == 0)
+    def _():
+        edge_up.wait_recv()
+        edge_up.wait_send()
+
+    @pl.when(z == NZ - 1)
+    def _():
+        edge_down.wait_recv()
+        edge_down.wait_send()
+
     edge_first.wait_recv()
     edge_last.wait_recv()
 
@@ -513,7 +529,7 @@
     for d in FAR_FIRST:
         q_copy(d).wait_send()
         g_copy(d).wait_send()
-    for copy in bulk + [edge_up, edge_down, edge_first, edge_last]:
+    for copy in bulk + [edge_first, edge_last]:
         copy.wait_send()
 
     @pl.when(has_prev)
@@ -576,13 +592,16 @@
 def update(pre, even, odd, packed, face, conserved, faces_out, co, fo, store_sem):
     lane = lanes((8, 128))
 
-    def copy(f):
-        return pltpu.make_async_copy(co.at[f], conserved.at[f], store_sem.at[f])
-
-    def face_copy(k):
-        return pltpu.make_async_copy(fo.at[k], faces_out.at[k], store_sem.at[FIELDS + k])
-
-    for f in range(FIELDS):
+    def stores(f, part):
+        at = pl.ds(PART * part, PART)
+        out = [pltpu.make_async_copy(co.at[f, at], conserved.at[f, at], store_sem.at[f, part])]
+        if f >= NV:
+            k = f - NV
+            out.append(pltpu.make_async_copy(fo.at[k, at], faces_out.at[k, at], store_sem.at[FIELDS + k, part]))
+        return out
+
+    order = (5, 6, 7, 0, 1, 2, 3, 4)
+    for f in order:
         shift = (120 - 16 * f) % 128
         delta = even if f % 2 == 0 else odd
 
@@ -598,15 +617,15 @@
                     fo[f - NV, r, at, 128:256] = jnp.where(lane >= 120, p, face[f - NV, r, at, 128:256])
             return carry
 
-        lax.fori_loop(0, ROWS, step, 0, unroll=8)
-        copy(f).start()
-        if f >= NV:
-            face_copy(f - NV).start()
-
-    for f in range(FIELDS):
-        copy(f).wait()
-    for k in range(NF):
-        face_copy(k).wait()
+        for part in range(ROWS // PART):
+            lax.fori_loop(PART * part, PART * part + PART, step, 0, unroll=8)
+            for store in stores(f, part):
+                store.start()
+
+    for f in order:
+        for part in range(ROWS // PART):
+            for store in stores(f, part):
+                store.wait()
 
 
 def run_update(pre, even, odd, packed, face):
@@ -621,7 +640,7 @@
         scratch_shapes=[
             pltpu.VMEM((FIELDS, ROWS, CELLS, THETA), F32),
             pltpu.VMEM((NF, ROWS, CELLS, THETA), F32),
-            pltpu.SemaphoreType.DMA((FIELDS + NF,)),
+            pltpu.SemaphoreType.DMA((FIELDS + NF, ROWS // PART)),
         ],
         compiler_params=pltpu.CompilerParams(vmem_limit_bytes=16 << 20),
         name="update",

time: 35.4 us -> 34.1 us (0.963)
  Pallas kernels: 34.7 us -> 33.3 us
    pallas_call x1, Pallas kernels: 3.96 us -> 2.95 us  [run_update(): pl.pallas_call(update, out_shape=(jax.ShapeDtypeStruct((FIELDS, ROWS, CEL...]
where the time goes in v4:
time: 34.1 us; the launch traced here: 34 us
  Pallas kernels  33.3 us (98%)
  between operations  0.65 us (2%)
    pallas_call x1, Pallas kernels, run_exchange(): pl.pallas_call(exchange, out_shape=(jax.ShapeDtypeStruct((FIELDS, ROWS, C...  30.4 us
    pallas_call x1, Pallas kernels, run_update(): pl.pallas_call(update, out_shape=(jax.ShapeDtypeStruct((FIELDS, ROWS, CEL...  2.95 us

profile of v4, /device:TPU:1, one launch (start us, length us, event | category | flops | bytes accessed | tf_op | source)
XLA Modules:
  0.0 34.0 jit_solution(14903453209237427519)
XLA Ops:
  0.6 0.0 copy-start
  0.6 30.4 %exchange.1 = (f32[8,32,16,256]{3,2,1,0:T(8,128)S(1)}, f32[32,16,128]{2,1,0:T(8,128)S(1)}, f32[32,16,128]{2,1,0:T(8,128)S(1)}, f32[32,16,128]{2,1,0:T(8,128)S(1)}) custom-call(s32[16]{0:T(128)} %widths_hbm.1, f32[5,32,16,256]{3,2,1,0:T(8,128)} %hydro.1, f32[3,32,16,256]{3,2,1,0:T(8,128)} %face.3, f32[5,256]{1,0:T(8,128)} %diffusion_hbm.1), custom_call_target="tpu_custom_call" | custom-call | tf_op jit(solution)/shard_map/exchange/pallas_call | solution.py:555
  31.0 0.0 copy-done
  31.0 2.9 %update.1 = (f32[8,32,16,256]{3,2,1,0:T(8,128)}, f32[3,32,16,256]{3,2,1,0:T(8,128)}) custom-call(f32[8,32,16,256]{3,2,1,0:T(8,128)S(1)} %get-tuple-element.6.pre, f32[32,16,128]{2,1,0:T(8,128)S(1)} %get-tuple-element.7.even, f32[32,16,128]{2,1,0:T(8,128)S(1)} %get-tuple-element.8.odd, f32[32,16,128]{2,1,0:T(8,128)S(1)} %get-tuple-element.9.packed, ...), custom_call_target="tpu_custom_call" | custom-call | tf_op jit(solution)/shard_map/update/pallas_call | solution.py:632
Async XLA Ops:
  0.6 30.4 %copy-start = (f32[3,32,16,256]{3,2,1,0:T(8,128)S(1)}, f32[3,32,16,256]{3,2,1,0:T(8,128)}, u32[]{:S(2)}) copy-start(f32[3,32,16,256]{3,2,1,0:T(8,128)} %face.3) | copy-start | bytes 4718596

commit v5 on v4

--- a/solution.py
+++ b/solution.py
@@ -13,6 +13,7 @@
 EARLY = 5
 BATCH = 8
 PART = 8
+G_ORDER = (5, 3, 7, 1, 6, 2, 4)
 FAR_FIRST = (4, 3, 5, 2, 6, 1, 7)
 
 
@@ -40,13 +41,18 @@
     dd, mm, widths, diffusion, small_sem,
     load_sem, q_send, q_recv, qn_send, qn_recv, qp_send, qp_recv,
     la_send, la_recv, e_send, e_recv, g_send, g_recv,
-    p_send, p_recv, r_send, r_recv,
+    p_send, p_recv, r_send, r_recv, fed, f_sem,
 ):
     row, phi = lax.axis_index("row"), lax.axis_index("phi")
     z, g = phi % NZ, phi // NZ
     nphi = NZ * NG
     after, before = (phi + 1) % nphi, (phi + nphi - 1) % nphi
     has_prev, has_next = row > 0, row < NROW - 1
+
+    at_seam = jnp.logical_or(z == 0, z == NZ - 1)
+    feeder = jnp.logical_or(z == 1, z == NZ - 2)
+    beside = g * NZ + z + 1 - 2 * (z % 2)
+    off_seam = jnp.logical_not(at_seam)
 
     def peer(d):
         return g * NZ + (z + d) % NZ
@@ -75,7 +81,11 @@
 
     for d in range(1, NZ):
         hello(row, peer(d))
-        hello(row, group(d))
+
+    @pl.when(off_seam)
+    def _():
+        for d in range(1, NG):
+            hello(row, group(d))
 
     @pl.when(has_prev)
     def _():
@@ -151,7 +161,7 @@
             copy.wait()
         pack(i, 0)
 
-    hellos = 2 * (NZ - 1) + NZ * (has_prev.astype(jnp.int32) + has_next.astype(jnp.int32))
+    hellos = (NZ - 1) + (NG - 1) * off_seam.astype(jnp.int32) + NZ * (has_prev.astype(jnp.int32) + has_next.astype(jnp.int32))
     hellos += (z == 0).astype(jnp.int32) + (z == NZ - 1).astype(jnp.int32)
     pl.semaphore_wait(barrier, hellos)
 
@@ -319,23 +329,29 @@
     def g_copy(d):
         return remote(gsum.at[g], gsum.at[g], g_send.at[d], g_recv.at[d], row, group(d))
 
-    for d in (5, 3, 7, 1, 6, 2, 4):
-        g_copy(d).start()
-
-    s32p, s64p = z_sums((z + NZ - 1) % NZ)
-    s32n, s64n = z_sums((z + 1) % NZ)
-    edge[0] = jnp.where(wide == 32, s32p * (1 / 32), s64p * (1 / 64))[:ROWS]
-    edge[1] = jnp.where(wide == 32, s32n * (1 / 32), s64n * (1 / 64))[:ROWS]
-    edge_up = remote(edge.at[0], edge.at[2], e_send.at[0], e_recv.at[0], row, group(1))
-    edge_down = remote(edge.at[1], edge.at[3], e_send.at[1], e_recv.at[1], row, group(NG - 1))
-
-    @pl.when(z == 0)
+    @pl.when(off_seam)
+    def _():
+        for d in G_ORDER:
+            g_copy(d).start()
+
+    def z_edge(at):
+        s32, s64 = z_sums(at)
+        return jnp.where(wide == 32, s32 * (1 / 32), s64 * (1 / 64))
+
+    edge[4] = z_edge(jnp.where(z == 1, NZ - 1, 0))
+    edge_up = remote(edge.at[4], edge.at[2], e_send.at[0], e_recv.at[0], row, group(1))
+    edge_down = remote(edge.at[4], edge.at[3], e_send.at[1], e_recv.at[1], row, group(NG - 1))
+
+    @pl.when(z == 1)
     def _():
         edge_up.start()
 
-    @pl.when(z == NZ - 1)
+    @pl.when(z == NZ - 2)
     def _():
         edge_down.start()
+
+    edge[0] = z_edge((z + NZ - 1) % NZ)
+    edge[1] = z_edge((z + 1) % NZ)
 
     for copy in bulk[2 * EARLY:]:
         copy.start()
@@ -437,15 +453,17 @@
         return carry
     lax.fori_loop(0, ROWS, face_step, 0, unroll=8)
 
-    for d in (5, 3, 7, 1, 6, 2, 4):
-        g_copy(d).wait_recv()
-
-    @pl.when(z == 0)
+    @pl.when(off_seam)
+    def _():
+        for d in G_ORDER:
+            g_copy(d).wait_recv()
+
+    @pl.when(z == 1)
     def _():
         edge_up.wait_recv()
         edge_up.wait_send()
 
-    @pl.when(z == NZ - 1)
+    @pl.when(z == NZ - 2)
     def _():
         edge_down.wait_recv()
         edge_down.wait_send()
@@ -468,13 +486,29 @@
 
     s32, s64 = z_sums(z)
     mm[0] = g_means(g, jnp.where(wide == 32, s32 * (1 / 32), s64 * (1 / 64)))
-    gp = jnp.where(z == 0, (g + NG - 1) % NG, g)
-    gn = jnp.where(z == NZ - 1, (g + 1) % NG, g)
-    pad = jnp.zeros((8, 128), F32)
-    ep = jnp.concatenate([jnp.where(z == 0, edge[2], edge[0]), pad])
-    en = jnp.concatenate([jnp.where(z == NZ - 1, edge[3], edge[1]), pad])
-    mm[1] = jnp.where(wide <= 16, jnp.concatenate([last_in[...], pad]), g_means(gp, ep))
-    mm[2] = jnp.where(wide <= 16, jnp.concatenate([first_in[...], pad]), g_means(gn, en))
+    mm[1] = g_means(g, edge[0])
+    mm[2] = g_means(g, edge[1])
+    feed = remote(fed.at[0], fed.at[1], f_sem.at[0], f_sem.at[1], row, beside)
+
+    @pl.when(feeder)
+    def _():
+        low_side = z == 1
+        across = g_means(
+            jnp.where(low_side, (g + NG - 1) % NG, (g + 1) % NG),
+            jnp.where(low_side, edge[2], edge[3]),
+        )
+        fed[0, 0] = jnp.where(low_side, mm[1], mm[2])
+        fed[0, 1] = jnp.where(low_side, across, mm[0])
+        fed[0, 2] = jnp.where(low_side, mm[0], across)
+        feed.start()
+
+    @pl.when(at_seam)
+    def _():
+        feed.wait_recv()
+        mm[...] = fed[1]
+
+    mm[1, 0:ROWS] = jnp.where(wide[:ROWS] <= 16, last_in[...], mm[1, 0:ROWS])
+    mm[2, 0:ROWS] = jnp.where(wide[:ROWS] <= 16, first_in[...], mm[2, 0:ROWS])
     narrow = width <= 16
 
     def differ(r, carry):
@@ -528,7 +562,13 @@
 
     for d in FAR_FIRST:
         q_copy(d).wait_send()
-        g_copy(d).wait_send()
+
+    @pl.when(off_seam)
+    def _():
+        for d in G_ORDER:
+            g_copy(d).wait_send()
+
+    pl.when(feeder)(feed.wait_send)
     for copy in bulk + [edge_first, edge_last]:
         copy.wait_send()
 
@@ -566,7 +606,7 @@
             pltpu.VMEM((ROWS, CELLS, 128), F32),
             pltpu.VMEM((NZ, ROWS + 8, 128), F32),
             pltpu.VMEM((NG, ROWS + 8, 128), F32),
-            pltpu.VMEM((4, ROWS, 128), F32),
+            pltpu.VMEM((5, ROWS + 8, 128), F32),
             pltpu.VMEM((ROWS, 128), F32),
             pltpu.VMEM((ROWS, 128), F32),
             pltpu.VMEM((ROWS, 128), F32),
@@ -581,6 +621,7 @@
             dma((NZ,)), dma((NZ,)), dma((NZ,)), dma((NZ,)), dma((NZ,)), dma((NZ,)),
             dma((4,)), dma((4,)), dma((2,)), dma((2,)), dma((NG,)), dma((NG,)),
             dma((2 * NV + 1,)), dma((2 * NV + 1,)), dma((3,)), dma((3,)),
+            pltpu.VMEM((2, 3, ROWS + 8, 128), F32), dma((2,)),
         ],
         compiler_params=pltpu.CompilerParams(
             collective_id=0, has_side_effects=True, vmem_limit_bytes=20 << 20

time: 34.1 us -> 32.2 us (0.944)
  Pallas kernels: 33.3 us -> 31.4 us
    pallas_call x1, Pallas kernels: 30.4 us -> 28.5 us  [run_exchange(): pl.pallas_call(exchange, out_shape=(jax.ShapeDtypeStruct((FIELDS, ROWS, C...]
where the time goes in v5:
time: 32.2 us; the launch traced here: 32.1 us
  Pallas kernels  31.4 us (98%)
  between operations  0.65 us (2%)
    pallas_call x1, Pallas kernels, run_exchange(): pl.pallas_call(exchange, out_shape=(jax.ShapeDtypeStruct((FIELDS, ROWS, C...  28.5 us
    pallas_call x1, Pallas kernels, run_update(): pl.pallas_call(update, out_shape=(jax.ShapeDtypeStruct((FIELDS, ROWS, CEL...  2.95 us

profile of v5, /device:TPU:1, one launch (start us, length us, event | category | flops | bytes accessed | tf_op | source)
XLA Modules:
  0.0 32.1 jit_solution(904713348221180089)
XLA Ops:
  0.6 0.0 copy-start
  0.6 28.5 %exchange.1 = (f32[8,32,16,256]{3,2,1,0:T(8,128)S(1)}, f32[32,16,128]{2,1,0:T(8,128)S(1)}, f32[32,16,128]{2,1,0:T(8,128)S(1)}, f32[32,16,128]{2,1,0:T(8,128)S(1)}) custom-call(s32[16]{0:T(128)} %widths_hbm.1, f32[5,32,16,256]{3,2,1,0:T(8,128)} %hydro.1, f32[3,32,16,256]{3,2,1,0:T(8,128)} %face.3, f32[5,256]{1,0:T(8,128)} %diffusion_hbm.1), custom_call_target="tpu_custom_call" | custom-call | tf_op jit(solution)/shard_map/exchange/pallas_call | solution.py:595
  29.1 0.0 copy-done
  29.1 2.9 %update.1 = (f32[8,32,16,256]{3,2,1,0:T(8,128)}, f32[3,32,16,256]{3,2,1,0:T(8,128)}) custom-call(f32[8,32,16,256]{3,2,1,0:T(8,128)S(1)} %get-tuple-element.6.pre, f32[32,16,128]{2,1,0:T(8,128)S(1)} %get-tuple-element.7.even, f32[32,16,128]{2,1,0:T(8,128)S(1)} %get-tuple-element.8.odd, f32[32,16,128]{2,1,0:T(8,128)S(1)} %get-tuple-element.9.packed, ...), custom_call_target="tpu_custom_call" | custom-call | tf_op jit(solution)/shard_map/update/pallas_call | solution.py:673
Async XLA Ops:
  0.6 28.5 %copy-start = (f32[3,32,16,256]{3,2,1,0:T(8,128)S(1)}, f32[3,32,16,256]{3,2,1,0:T(8,128)}, u32[]{:S(2)}) copy-start(f32[3,32,16,256]{3,2,1,0:T(8,128)} %face.3) | copy-start | bytes 4718596
